TPU v7x, 128 devices: a whole 4x4x4 slice. The times are simulated.
128 devices in a mesh: row: 16 (over x, z_lo, core), col: 8 (over y, z_hi).
Axes of the slice: x: 4, y: 4, z: 4 (z_hi: 2, z_lo: 2; z = z_hi * 2 + z_lo), core: 2. Of those that a mesh axis runs over, the one named last changes fastest.
Arguments:
- schur_tail: float32 [1024, 1024], P(('row', 'col')), as said below
- coupling: float32 [1024, 16384], P(None, 'row'), may hold values from -4 to 4
- ks_lead: float32 [16384, 4096], P('row', 'col'), may hold values from -0.046875 to 0.046875
- ks_tail: float32 [1024, 4096], P('row', 'col'), may hold values from -0.046875 to 0.046875
- inv_mask: int32 [8, 136], replicated, may hold values 0 or 1
- ks_mask: int32 [136, 32], replicated, may hold values 0 or 1
Outputs:
- projected: float32 [1024, 4096], P('row', 'col')
Inputs may be any that keep to these rules, and one draw needn't show every extreme that they name: `schur_tail`: symmetric and positive definite, with diagonal entries between about 1 and 32.
All inputs are finite; a program needn't handle non-finite values.
Results may differ from a plain program's by a relative error of at most 0.00009.
Values sent between devices are 32-bit elements; how exact they have to be, the bound alone decides.
No kernel may reach another device: no remote copies, remote signals or barrier semaphores. Data moves between devices by JAX's collectives and lax.ppermute only.
A program may use at most 128 MiB of HBM per device.

v0:
```python
import jax
import jax.numpy as jnp
from jax import lax
from jax.experimental import pallas as pl
from jax.experimental.pallas import tpu as pltpu
from jax.sharding import Mesh
from jax.sharding import PartitionSpec as P

BLK = 128
ROW = ("row_0", "row_1", "row_2")
COL = ("col_0", "col_1")
ROW_COL = ROW + COL
CHIPS = ("row_0", "row_1", "col_0", "col_1")
F32 = jnp.float32
BF16 = jnp.bfloat16
SENT = 5


def dot_bf16(a, b):
    return jnp.dot(a, b, preferred_element_type=F32)


def halves(x):
    high = x.astype(BF16)
    return high, (x - high.astype(F32)).astype(BF16)


def dot_three(a, b_high, b_low):
    high, low = halves(a)
    return dot_bf16(high, b_high) + (dot_bf16(high, b_low) + dot_bf16(low, b_high))


def lane_copy(x, column):
    return jnp.take_along_axis(x, jnp.full((8, BLK), column, jnp.int32), axis=1)


def row_copy(x, row):
    return jnp.broadcast_to(x[row : row + 1, :], (8, BLK))


def factor_panels(rows, sub, lane):
    groups = len(rows)
    late = []

    def flush(chosen):
        for g, update in [item for item in late if item[0] in chosen]:
            update()
        late[:] = [item for item in late if item[0] not in chosen]

    for t in range(0, groups, 2):
        first = 8 * t
        flush((t, t + 1))
        pivot = [[], []]
        for m in range(16):
            for y in range(2):
                pivot[y].append(lane_copy(rows[t + y], first + m))
        below = {g: [] for g in range(t + 2, groups)}
        near = [g for g in below if g < t + 4]
        flush(near)
        for m in range(16):
            for g in near:
                below[g].append(lane_copy(rows[g], first + m))
        flush(range(groups))
        for m in range(16):
            for g in range(t + 4, groups):
                below[g].append(lane_copy(rows[g], first + m))
        here = (lane >= first) & (lane < first + 16)
        full = [
            jnp.where(here, jnp.where(lane - first - 8 * y == sub, 1.0, 0.0), rows[t + y])
            for y in range(2)
        ]
        result = list(full)
        inverses = []
        for k in range(0, 16, 2):
            x, i = k // 8, k % 8
            a = row_copy(pivot[x][k], i)
            b = row_copy(pivot[x][k + 1], i)
            c = row_copy(pivot[x][k + 1], i + 1)
            det = a * c - b * b
            root = lax.rsqrt(det)
            q = root * root
            left = []
            for y in range(2):
                u, v = pivot[y][k], pivot[y][k + 1]
                u, v = u * c - v * b, v * a - u * b
                if y == x:
                    others = (sub < i) | (sub > i + 1)
                    u, v = jnp.where(others, u, 0.0), jnp.where(others, v, 0.0)
                left.append((u, v))
            for m in range(k + 2, 16):
                top, low = row_copy(pivot[x][m], i), row_copy(pivot[x][m], i + 1)
                for y in range(2):
                    pivot[y][m] = pivot[y][m] - (left[y][0] * top + left[y][1] * low) * q
            top, low = row_copy(full[x], i), row_copy(full[x], i + 1)
            for y in range(2):
                full[y] = full[y] - (left[y][0] * top + left[y][1] * low) * q
            root_a = lax.rsqrt(a)
            over_a = root_a * root_a
            root_c = lax.rsqrt(det * over_a)
            result[x] = jnp.where(
                sub == i,
                top * root_a,
                jnp.where(sub == i + 1, (low - b * over_a * top) * root_c, result[x]),
            )
            inverses.append((q * a, q * b, q * c))
        rows[t], rows[t + 1] = result
        if below:
            lines = []
            for k in range(0, 16, 2):
                qa, qb, qc = inverses[k // 2]
                top = row_copy(full[k // 8], k % 8)
                low = row_copy(full[k // 8], k % 8 + 1)
                lines += [qc * top - qb * low, qa * low - qb * top]

            def update(g, lines=lines, below=below, here=here):
                terms = [a * b for a, b in zip(below[g], lines)]
                while len(terms) > 1:
                    terms = [a + b for a, b in zip(terms[::2], terms[1::2])]
                rows[g] = jnp.where(here, 0.0, rows[g]) - terms[0]

            for g in below:
                if g in near:
                    update(g)
                else:
                    late.append((g, lambda g=g, update=update: update(g)))
        yield


def kernel(
    where_ref, inv_mask, ks_mask, mine_ref, other_ref, coupling_hbm, lead_hbm, tail_hbm,
    kept_ref, sent_ref,
    m_ref, coupling_ref, lead_ref, tail_ref, ch_ref, cl_ref, kh_ref, kl_ref, th_ref, tl_ref,
    before_ref, right_even, right_odd, left_ref, sem, strip_sem,
):
    right_refs = (right_even, right_odd)
    size = m_ref.shape[0]
    count = size // BLK
    row, col, core = where_ref[0], where_ref[1], where_ref[2]
    copies = [
        pltpu.make_async_copy(coupling_hbm, coupling_ref, sem.at[0]),
        pltpu.make_async_copy(lead_hbm, lead_ref, sem.at[1]),
        pltpu.make_async_copy(tail_hbm, tail_ref, sem.at[2]),
    ]
    sub = lax.broadcasted_iota(jnp.int32, (8, BLK), 0)
    lane = lax.broadcasted_iota(jnp.int32, (8, BLK), 1)

    def at(i):
        return slice(i * BLK, (i + 1) * BLK)

    strips = {b: [] for b in range(count)}
    folds = {b: [] for b in range(count)}
    sems = iter(range(strip_sem.shape[0]))
    for b in range(count):
        for ref, part in ((mine_ref, core), (other_ref, 1 - core)):
            held = pl.ds(pl.multiple_of(b * BLK + part * 64, 64), 64)
            direct = min(SENT, count - b) * BLK
            strips[b].append(
                pltpu.make_async_copy(
                    ref.at[b, :, pl.ds(0, direct)],
                    m_ref.at[held, pl.ds(b * BLK, direct)],
                    strip_sem.at[next(sems)],
                )
            )
            for o in range(count - b, SENT - 1):
                c = b + o - count
                strips[b].append(
                    pltpu.make_async_copy(
                        ref.at[b, :, pl.ds(o * BLK, BLK)],
                        m_ref.at[held, pl.ds(c * BLK, BLK)],
                        strip_sem.at[next(sems)],
                    )
                )
    for b in range(count):
        for copy in strips[b]:
            copy.start()
    for copy in copies:
        copy.start()
    for copy in strips[0]:
        copy.wait()

    def arrive():
        for b in range(1, count):
            for copy in strips[b]:
                copy.wait()
        yield
        for b in range(SENT, count):
            for c in range(b - SENT + 1):
                m_ref[at(c), at(b)] = m_ref[at(b), at(c)].T
            yield

    def prepare():
        for copy in copies:
            copy.wait()
        for k in range(count):
            ch_ref[at(k), :], cl_ref[at(k), :] = halves(coupling_ref[at(k), :])
            yield
        for k in range(count):
            for n in range(lead_ref.shape[1] // BLK):
                keep = ks_mask[row * count + k, col * 4 + n].astype(F32)
                kh_ref[at(k), at(n)], kl_ref[at(k), at(n)] = halves(lead_ref[at(k), at(n)] * keep)
            yield
        th_ref[...] = jnp.zeros(th_ref.shape, BF16)
        tl_ref[...] = jnp.zeros(tl_ref.shape, BF16)
        lead_blocks = ks_mask.shape[0] - count
        for n in range(lead_ref.shape[1] // BLK):
            keep = ks_mask[lead_blocks + row // 2, col * 4 + n].astype(F32)
            high, low = halves(tail_ref[:, at(n)] * keep)
            th_ref[pl.ds(core * 64, 64), at(n)] = high
            tl_ref[pl.ds(core * 64, 64), at(n)] = low
        yield

    def stack(ref, cols, value):
        high, low = halves(value)
        ref[0:BLK, cols] = high
        ref[BLK : 2 * BLK, cols] = high
        ref[2 * BLK :, cols] = low

    def beside(value):
        high, low = halves(value)
        return jnp.concatenate([high, low, high], axis=1)

    def eliminate(j, i, parts):
        right = right_refs[j % 2]
        left = left_ref[i]
        for cols in parts:
            start, stop = cols.start, cols.stop
            update = dot_bf16(left, right[:, cols])
            if start == j * BLK and stop == start + BLK:
                m_ref[at(i), cols] = -update
            else:
                m_ref[at(i), cols] -= update

    def prepare_row(j):
        if j > 0:
            stack(before_ref, slice(0, j * BLK), m_ref[at(j), : j * BLK])
            yield
        if j + 1 < count:
            stack(before_ref, slice((j + 1) * BLK, size), m_ref[at(j), (j + 1) * BLK :])
            yield

    def trailing(j, i, first):
        if not first:
            left_ref[i] = beside(m_ref[at(j), at(i)].T)
        parts = [slice(c * BLK, (c + 1) * BLK) for c in (j,)]
        if j > 0:
            parts.append(slice(0, j * BLK))
        start = (i + 1 if first else i) * BLK
        if start < size:
            parts.append(slice(start, size))
        for part in parts:
            eliminate(j, i, [part])
            yield

    def project(i):
        depth = slice(0, (i + 1) * BLK)
        right = right_refs[i % 2]
        high, low = right[0:BLK, depth], right[2 * BLK :, depth]
        total = None
        for k in range(0, count, 2):
            wide = slice(k * BLK, (k + 2) * BLK)
            lead = dot_bf16(high, ch_ref[depth, wide]) + (
                dot_bf16(high, cl_ref[depth, wide]) + dot_bf16(low, ch_ref[depth, wide])
            )
            keep = [inv_mask[i, row * count + k + q].astype(F32) for q in range(2)]
            lead = jnp.concatenate([lead[:, :BLK] * keep[0], lead[:, BLK:] * keep[1]], axis=1)
            part = dot_three(lead, kh_ref[wide, :], kl_ref[wide, :])
            total = part if total is None else total + part
            yield
        mine = m_ref[at(i), pl.ds(pl.multiple_of(row // 2 * BLK, BLK), BLK)]
        keep = inv_mask[i, inv_mask.shape[1] - count + row // 2]
        mine = jnp.where((keep != 0) & (row // 2 <= i), mine, 0.0)
        total = dot_three(mine, th_ref[...], tl_ref[...]) - total
        half = BLK // 2
        kept_ref[i] = jnp.where(core == 0, total[:half], total[half:])
        sent_ref[i] = jnp.where(core == 0, total[half:], total[:half])
        yield

    fillers = [arrive(), prepare_row(0), prepare()]
    for j in range(count):
        rows = [m_ref[j * BLK + 8 * g : j * BLK + 8 * g + 8, at(j)] for g in range(16)]
        for step in factor_panels(rows, sub, lane):
            for _ in range(5):
                while fillers:
                    try:
                        next(fillers[0])
                        break
                    except StopIteration:
                        fillers.pop(0)
        while fillers:
            for _ in fillers.pop(0):
                pass
        p = jnp.concatenate([jnp.where(lane <= sub + 8 * g, rows[g], 0.0) for g in range(16)], axis=0)
        right = right_refs[j % 2]
        left = beside(p)
        m_ref[at(j), at(j)] = p
        stack(right, at(j), p)
        if j + 1 < count:
            u = dot_bf16(left, before_ref[:, at(j + 1)])
            m_ref[at(j), at(j + 1)] = u
            stack(right, at(j + 1), u)
            left_ref[j + 1] = beside(u.T)
            eliminate(j, j + 1, [at(j + 1)])
        spans = [slice(0, j * BLK)] if j > 0 else []
        if j + 2 < count:
            spans.append(slice((j + 2) * BLK, size))
        for span in spans:
            u = dot_bf16(left, before_ref[:, span])
            m_ref[at(j), span] = u
            stack(right, span, u)
        fillers = []
        if j + 1 < count:
            fillers += [trailing(j, j + 1, True), prepare_row(j + 1)]
        fillers += [trailing(j, i, False) for i in range(j + 2, count)] + [project(j)]
    while fillers:
        for _ in fillers.pop(0):
            pass


def projected_part(place, inv_mask, ks_mask, mine, other, coupling, ks_lead, ks_tail):
    size = coupling.shape[0]
    lead, width = ks_lead.shape
    vmem = pl.BlockSpec(memory_space=pltpu.VMEM)
    smem = pl.BlockSpec(memory_space=pltpu.SMEM)
    hbm = pl.BlockSpec(memory_space=pl.ANY)
    return pl.pallas_call(
        kernel,
        out_shape=[jax.ShapeDtypeStruct((size // BLK, BLK // 2, width), F32)] * 2,
        in_specs=[smem, smem, smem, hbm, hbm, hbm, hbm, hbm],
        out_specs=[vmem, vmem],
        scratch_shapes=[
            pltpu.VMEM((size, size), F32),
            pltpu.VMEM(coupling.shape, F32),
            pltpu.VMEM(ks_lead.shape, F32),
            pltpu.VMEM(ks_tail.shape, F32),
            pltpu.VMEM(coupling.shape, BF16),
            pltpu.VMEM(coupling.shape, BF16),
            pltpu.VMEM(ks_lead.shape, BF16),
            pltpu.VMEM(ks_lead.shape, BF16),
            pltpu.VMEM((BLK, width), BF16),
            pltpu.VMEM((BLK, width), BF16),
            pltpu.VMEM((3 * BLK, size), BF16),
            pltpu.VMEM((3 * BLK, size), BF16),
            pltpu.VMEM((3 * BLK, size), BF16),
            pltpu.VMEM((size // BLK, BLK, 3 * BLK), BF16),
            pltpu.SemaphoreType.DMA((3,)),
            pltpu.SemaphoreType.DMA((28,)),
        ],
        compiler_params=pltpu.CompilerParams(vmem_limit_bytes=48 * 1024 * 1024),
        name="project",
    )(place, inv_mask, ks_mask, mine, other, coupling, ks_lead, ks_tail)


def pieces_first(where_ref, kept, got, z_kept, z_sent, x_own, *x_sent):
    x, z = where_ref[0], where_ref[1]
    half = kept.shape[-1] // 2
    lo, hi = slice(0, half), slice(half, 2 * half)
    for i in range(4):
        z_kept[i] = kept[2 * i + z, :, lo] + got[2 * i + z, :, lo]
        z_sent[i] = kept[2 * i + 1 - z, :, lo] + got[2 * i + 1 - z, :, lo]
    for k, ref in enumerate((x_own, *x_sent)):
        to = lax.rem(x + k, 4)
        for i in range(2):
            ref[i] = kept[2 * to + i, :, hi] + got[2 * to + i, :, hi]


def pieces_second(where_ref, z_kept, z_got, x_own, x1, x2, x3, y_own, y1, y2, y3, v_kept, v_sent):
    x, z = where_ref[0], where_ref[1]
    for k, ref in enumerate((y_own, y1, y2, y3)):
        to = lax.rem(x + k, 4)
        ref[...] = z_kept[to] + z_got[to]
    for ref, i in ((v_kept, z), (v_sent, 1 - z)):
        ref[...] = (x_own[i] + x1[i]) + (x2[i] + x3[i])


def pieces_third(y_own, y1, y2, y3, v_kept, v_got, out):
    half = out.shape[-1] // 2
    out[:, :half] = (y_own[...] + y1[...]) + (y2[...] + y3[...])
    out[:, half:] = v_kept[...] + v_got[...]


def summed(where, kept, sent):
    vmem = pl.BlockSpec(memory_space=pltpu.VMEM)
    smem = pl.BlockSpec(memory_space=pltpu.SMEM)
    swap = [(0, 1), (1, 0)]
    rows, half = kept.shape[1], kept.shape[2] // 2

    def shape(*lead):
        return jax.ShapeDtypeStruct((*lead, rows, half), F32)

    def turned(parts):
        return [
            lax.ppermute(part, "row_0", [(s, (s + k) % 4) for s in range(4)])
            for k, part in zip((1, 2, 3), parts)
        ]

    got = lax.ppermute(sent, "row_2", swap)
    z_kept, z_sent, x_own, *x_sent = pl.pallas_call(
        pieces_first,
        out_shape=[shape(4), shape(4)] + [shape(2)] * 4,
        in_specs=[smem, vmem, vmem],
        out_specs=[vmem] * 6,
        name="pieces_first",
    )(where, kept, got)
    z_got = lax.ppermute(z_sent, "row_1", swap)
    x_got = turned(x_sent)
    y_own, y1, y2, y3, v_kept, v_sent = pl.pallas_call(
        pieces_second,
        out_shape=[shape()] * 6,
        in_specs=[smem] + [vmem] * 6,
        out_specs=[vmem] * 6,
        name="pieces_second",
    )(where, z_kept, z_got, x_own, *x_got)
    v_got = lax.ppermute(v_sent, "row_1", swap)
    y_got = turned((y1, y2, y3))
    return pl.pallas_call(
        pieces_third,
        out_shape=jax.ShapeDtypeStruct((rows, 2 * half), F32),
        in_specs=[vmem] * 6,
        out_specs=vmem,
        name="pieces_third",
    )(y_own, *y_got, v_kept, v_got)


def per_device(schur_tail, coupling, ks_lead, ks_tail, inv_mask, ks_mask):
    row_index = lax.axis_index(ROW)
    col_index = lax.axis_index(COL)
    core_index = lax.axis_index("row_2")
    twice = jnp.concatenate([schur_tail, schur_tail[:, : SENT * BLK - BLK]], axis=1)
    strip = lax.dynamic_slice_in_dim(twice, row_index // 2 * BLK, SENT * BLK, 1)
    chips = 1
    for axis in CHIPS:
        chips *= lax.axis_size(axis)
    copies = jnp.broadcast_to(strip[None], (chips,) + strip.shape)
    mine = lax.all_to_all(copies, CHIPS, split_axis=0, concat_axis=0, tiled=True)
    mine = mine.reshape(-1, BLK // 2, SENT * BLK)
    other = lax.ppermute(mine, "row_2", [(0, 1), (1, 0)])
    place = jnp.stack([row_index, col_index, core_index]).astype(jnp.int32)
    kept, sent = projected_part(place, inv_mask, ks_mask, mine, other, coupling, ks_lead, ks_tail)
    where = jnp.stack([lax.axis_index("row_0"), lax.axis_index("row_1")]).astype(jnp.int32)
    return summed(where, kept, sent)


def solution(mesh):
    split = Mesh(mesh.devices.reshape(4, 2, 2, 4, 2), ROW_COL)
    return jax.shard_map(
        per_device,
        mesh=split,
        in_specs=(P(ROW_COL, None), P(None, ROW), P(ROW, COL), P(ROW, COL), P(), P()),
        out_specs=P(ROW, COL),
        check_vma=False,
    )
```

profile of v0, /device:TPU:2, one launch (start us, length us, event | category | flops | bytes accessed | tf_op | source)
XLA Modules:
  0.0 104.0 jit_solution(200941060891445242)
XLA Ops:
  0.0 0.7 slice.3
  0.7 0.7 fusion
  1.5 0.1 broadcast_in_dim.2
  1.6 0.0 copy-start.12
  1.6 0.0 copy-start.1
  1.6 0.0 copy-start.2
  1.6 32.1 %all_to_all.5 = f32[64,8,640]{2,1,0:T(8,128)S(1)} all-to-all(f32[64,8,640]{2,1,0:T(8,128)S(1)} %broadcast_in_dim.2), channel_id=1, replica_groups=mesh['row_0'=4,'row_1'=2,'row_2'=2,'col_0'=4,'col_1'=2] {'row_0','row_1'..., dimensions={0} | all-to-all | bytes 2621440 | tf_op jit(solution)/shard_map/all_to_all | solution.py:434
  33.7 0.0 collective-permute-start
  33.7 0.0 copy-done.12
  33.7 0.1 copy.7.ks_mask
  33.8 0.1 pad_add_fusion.1.where_ref
  33.9 2.9 %collective-permute-done.other_ref = f32[8,64,640]{2,1,0:T(8,128)S(1)} collective-permute-done((f32[8,64,640]{2,1,0:T(8,128)S(1)}, f32[8,64,640]{2,1,0:T(8,128)S(1)}, u32[]{:S(2)}, u32[]{:S(2)}) %collective-permute-start) | collective-permute-done | bytes 1310752 | tf_op jit(solution)/shard_map/ppermute | solution.py:436
  36.7 0.0 copy-done.1
  36.7 0.0 copy-done.2
  36.7 34.6 %project.1 = (f32[8,64,512]{2,1,0:T(8,128)S(1)}, f32[8,64,512]{2,1,0:T(8,128)S(1)}) custom-call(s32[3]{0:T(128)S(1)} %pad_add_fusion.1.where_ref, s32[8,136]{1,0:T(8,128)S(1)} %copy-done.2, s32[136,32]{1,0:T(8,128)S(1)} %copy.7.ks_mask, f32[8,64,640]{2,1,0:T(8,128)S(1)} %bitcast.7, f32[8,64,640]{2,1,0:T(8,128)S(1)} %collective-permute-done.other_ref, ...), custom_call_target="tpu_custom_call" | custom-call | tf_op jit(solution)/shard_map/project/pallas_call | solution.py:325
  71.4 0.0 copy-start
  71.4 1.0 copy-done
  72.4 0.1 collective-permute-start.1
  72.5 0.7 pad_add_fusion.where_ref
  73.2 1.9 %collective-permute-done.1.got = f32[8,64,512]{2,1,0:T(8,128)S(1)} collective-permute-done((f32[8,64,512]{2,1,0:T(8,128)S(1)}, f32[8,64,512]{2,1,0:T(8,128)S(1)}, u32[]{:S(2)}, u32[]{:S(2)}) %collective-permute-start.1) | collective-permute-done | bytes 1048608 | tf_op jit(solution)/shard_map/ppermute | solution.py:396
  75.0 0.0 copy-start.3
  75.0 1.0 copy-done.3
  76.0 2.6 %pieces_first.1 = (f32[4,64,256]{2,1,0:T(8,128)}, f32[4,64,256]{2,1,0:T(8,128)}, f32[2,64,256]{2,1,0:T(8,128)}, f32[2,64,256]{2,1,0:T(8,128)}, f32[2,64,256]{2,1,0:T(8,128)}, /*index=5*/f32[2,64,256]{2,1,0:T(8,128)}) custom-call(s32[2]{0:T(128)} %pad_add_fusion.where_ref, f32[8,64,512]{2,1,0:T(8,128)} %copy-done, f32[8,64,512]{2,1,0:T(8,128)} %copy-done.3), custom_call_target="tpu_custom_call" | custom-call | tf_op jit(solution)/shard_map/pieces_first/pallas_call | solution.py:397
  78.6 0.0 collective-permute-start.2
  78.6 0.7 collective-permute-start.3
  79.4 2.7 %collective-permute-start.4 = (f32[2,64,256]{2,1,0:T(8,128)}, f32[2,64,256]{2,1,0:T(8,128)S(1)}, u32[]{:S(2)}, u32[]{:S(2)}) collective-permute-start(f32[2,64,256]{2,1,0:T(8,128)} %get-tuple-element.25), channel_id=1, source_target_pairs={{0,64},{32,96},{64,0},{96,32},{1,65},{33,97},{65,1},{97,33},{2,66}... | collective-permute-start | bytes 393224 | tf_op jit(solution)/shard_map/ppermute | solution.py:392
  82.0 0.5 collective-permute-start.5
  82.5 2.7 %collective-permute-done.3.x1 = f32[2,64,256]{2,1,0:T(8,128)S(1)} collective-permute-done((f32[2,64,256]{2,1,0:T(8,128)}, f32[2,64,256]{2,1,0:T(8,128)S(1)}, u32[]{:S(2)}, u32[]{:S(2)}) %collective-permute-start.3) | collective-permute-done | bytes 131104 | tf_op jit(solution)/shard_map/ppermute | solution.py:392
  85.2 0.0 copy-start.5
  85.2 2.2 %collective-permute-done.4.x2 = f32[2,64,256]{2,1,0:T(8,128)S(1)} collective-permute-done((f32[2,64,256]{2,1,0:T(8,128)}, f32[2,64,256]{2,1,0:T(8,128)S(1)}, u32[]{:S(2)}, u32[]{:S(2)}) %collective-permute-start.4) | collective-permute-done | bytes 131104 | tf_op jit(solution)/shard_map/ppermute | solution.py:392
  87.5 0.0 copy-start.6
  87.5 1.4 %collective-permute-done.5.x3 = f32[2,64,256]{2,1,0:T(8,128)S(1)} collective-permute-done((f32[2,64,256]{2,1,0:T(8,128)}, f32[2,64,256]{2,1,0:T(8,128)S(1)}, u32[]{:S(2)}, u32[]{:S(2)}) %collective-permute-start.5) | collective-permute-done | bytes 131104 | tf_op jit(solution)/shard_map/ppermute | solution.py:392
  88.9 0.0 copy-start.7
  88.9 0.0 collective-permute-done.2.z_got
  88.9 0.0 copy-start.4
  88.9 0.0 copy-done.5
  88.9 0.0 copy-done.6
  88.9 0.6 copy-done.7
  89.5 0.1 copy-done.4
  89.6 2.0 %pieces_second.1 = (f32[64,256]{1,0:T(8,128)}, f32[64,256]{1,0:T(8,128)}, f32[64,256]{1,0:T(8,128)}, f32[64,256]{1,0:T(8,128)}, f32[64,256]{1,0:T(8,128)}, /*index=5*/f32[64,256]{1,0:T(8,128)}) custom-call(s32[2]{0:T(128)} %pad_add_fusion.where_ref, f32[4,64,256]{2,1,0:T(8,128)} %get-tuple-element.21.z_kept, f32[4,64,256]{2,1,0:T(8,128)} %copy-done.4, ...), custom_call_target="tpu_custom_call" | custom-call | tf_op jit(solution)/shard_map/pieces_second/pallas_call | solution.py:406
  91.7 0.6 collective-permute-start.6
  92.2 3.0 %collective-permute-start.7 = (f32[64,256]{1,0:T(8,128)}, f32[64,256]{1,0:T(8,128)S(1)}, u32[]{:S(2)}, u32[]{:S(2)}) collective-permute-start(f32[64,256]{1,0:T(8,128)} %get-tuple-element.29), channel_id=1, source_target_pairs={{0,64},{32,96},{64,0},{96,32},{1,65},{33,97},{65,1},{97,33},{2,66}... | collective-permute-start | bytes 196616 | tf_op jit(solution)/shard_map/ppermute | solution.py:392
  95.2 2.0 %collective-permute-start.8 = (f32[64,256]{1,0:T(8,128)}, f32[64,256]{1,0:T(8,128)S(1)}, u32[]{:S(2)}, u32[]{:S(2)}) collective-permute-start(f32[64,256]{1,0:T(8,128)} %get-tuple-element.30), channel_id=1, source_target_pairs={{0,96},{32,0},{64,32},{96,64},{1,97},{33,1},{65,33},{97,65},{2,98}... | collective-permute-start | bytes 196616 | tf_op jit(solution)/shard_map/ppermute | solution.py:392
  97.2 1.6 %collective-permute-start.9 = (f32[64,256]{1,0:T(8,128)}, f32[64,256]{1,0:T(8,128)S(1)}, u32[]{:S(2)}, u32[]{:S(2)}) collective-permute-start(f32[64,256]{1,0:T(8,128)} %get-tuple-element.32), channel_id=1, source_target_pairs={{0,16},{16,0},{1,17},{17,1},{2,18},{18,2},{3,19},{19,3},{4,20},{20... | collective-permute-start | bytes 196616 | tf_op jit(solution)/shard_map/ppermute | solution.py:413
  98.8 0.0 collective-permute-done.6.y1
  98.8 0.0 copy-start.8
  98.8 0.0 collective-permute-done.7.y2
  98.8 0.0 copy-start.9
  98.8 0.8 collective-permute-done.8.y3
  99.7 0.0 copy-start.10
  99.7 2.0 %collective-permute-done.9.v_got = f32[64,256]{1,0:T(8,128)S(1)} collective-permute-done((f32[64,256]{1,0:T(8,128)}, f32[64,256]{1,0:T(8,128)S(1)}, u32[]{:S(2)}, u32[]{:S(2)}) %collective-permute-start.9) | collective-permute-done | bytes 65568 | tf_op jit(solution)/shard_map/ppermute | solution.py:413
  101.7 0.0 copy-start.11
  101.7 0.0 copy-done.8
  101.7 0.0 copy-done.9
  101.7 0.0 copy-done.10
  101.7 0.6 copy-done.11
  102.3 1.7 %pieces_third.1 = f32[64,512]{1,0:T(8,128)} custom-call(f32[64,256]{1,0:T(8,128)} %get-tuple-element.27.y_own, f32[64,256]{1,0:T(8,128)} %copy-done.8, f32[64,256]{1,0:T(8,128)} %copy-done.9, f32[64,256]{1,0:T(8,128)} %copy-done.10, f32[64,256]{1,0:T(8,128)} %get-tuple-element.31.v_kept, f32[64,256]{1,0:T(8,128)} %copy-done.11), custom_call_target="tpu_custom_call" | custom-call | tf_op jit(solution)/shard_map/pieces_third/pallas_call | solution.py:415
Async XLA Ops:
  1.6 32.1 %copy-start.12 = (s32[136,32]{0,1:T(8,128)S(1)}, s32[136,32]{0,1:T(8,128)}, u32[]{:S(2)}) copy-start(s32[136,32]{0,1:T(8,128)} %param.11) | copy-start | bytes 52228
  1.6 35.1 %copy-start.1 = (f32[64,512]{1,0:T(8,128)S(1)}, f32[64,512]{1,0:T(8,128)}, u32[]{:S(2)}) copy-start(f32[64,512]{1,0:T(8,128)} %tail_hbm.1) | copy-start | bytes 393220
  1.6 35.1 %copy-start.2 = (s32[8,136]{1,0:T(8,128)S(1)}, s32[8,136]{1,0:T(8,128)}, u32[]{:S(2)}) copy-start(s32[8,136]{1,0:T(8,128)} %inv_mask.1) | copy-start | bytes 13060
  33.7 3.0 %collective-permute-start = (f32[8,64,640]{2,1,0:T(8,128)S(1)}, f32[8,64,640]{2,1,0:T(8,128)S(1)}, u32[]{:S(2)}, u32[]{:S(2)}) collective-permute-start(f32[8,64,640]{2,1,0:T(8,128)S(1)} %bitcast.6), channel_id=1, source_target_pairs={{0,8},{8,0},{1,9},{9,1},{2,10},{10,2},{3,11},{11,3},{4,12},{12,4},... | collective-permute-start | bytes 3932168 | tf_op jit(solution)/shard_map/ppermute | solution.py:436
  71.4 1.0 copy-start
  72.4 2.7 %collective-permute-start.1 = (f32[8,64,512]{2,1,0:T(8,128)S(1)}, f32[8,64,512]{2,1,0:T(8,128)S(1)}, u32[]{:S(2)}, u32[]{:S(2)}) collective-permute-start(f32[8,64,512]{2,1,0:T(8,128)S(1)} %get-tuple-element.20), channel_id=1, source_target_pairs={{0,8},{8,0},{1,9},{9,1},{2,10},{10,2},{3,11},{11,3},{4,12},{12,4},... | collective-permute-start | bytes 3145736 | tf_op jit(solution)/shard_map/ppermute | solution.py:396
  75.0 1.0 copy-start.3
  78.6 10.3 %collective-permute-start.2 = (f32[4,64,256]{2,1,0:T(8,128)}, f32[4,64,256]{2,1,0:T(8,128)S(1)}, u32[]{:S(2)}, u32[]{:S(2)}) collective-permute-start(f32[4,64,256]{2,1,0:T(8,128)} %get-tuple-element.22), channel_id=1, source_target_pairs={{0,16},{16,0},{1,17},{17,1},{2,18},{18,2},{3,19},{19,3},{4,20},{20... | collective-permute-start | bytes 786440 | tf_op jit(solution)/shard_map/ppermute | solution.py:404
  78.6 6.6 %collective-permute-start.3 = (f32[2,64,256]{2,1,0:T(8,128)}, f32[2,64,256]{2,1,0:T(8,128)S(1)}, u32[]{:S(2)}, u32[]{:S(2)}) collective-permute-start(f32[2,64,256]{2,1,0:T(8,128)} %get-tuple-element.24), channel_id=1, source_target_pairs={{0,32},{32,64},{64,96},{96,0},{1,33},{33,65},{65,97},{97,1},{2,34}... | collective-permute-start | bytes 393224 | tf_op jit(solution)/shard_map/ppermute | solution.py:392
  79.4 8.1 %collective-permute-start.4 = (f32[2,64,256]{2,1,0:T(8,128)}, f32[2,64,256]{2,1,0:T(8,128)S(1)}, u32[]{:S(2)}, u32[]{:S(2)}) collective-permute-start(f32[2,64,256]{2,1,0:T(8,128)} %get-tuple-element.25), channel_id=1, source_target_pairs={{0,64},{32,96},{64,0},{96,32},{1,65},{33,97},{65,1},{97,33},{2,66}... | collective-permute-start | bytes 393224 | tf_op jit(solution)/shard_map/ppermute | solution.py:392
  82.0 6.8 %collective-permute-start.5 = (f32[2,64,256]{2,1,0:T(8,128)}, f32[2,64,256]{2,1,0:T(8,128)S(1)}, u32[]{:S(2)}, u32[]{:S(2)}) collective-permute-start(f32[2,64,256]{2,1,0:T(8,128)} %get-tuple-element.26), channel_id=1, source_target_pairs={{0,96},{32,0},{64,32},{96,64},{1,97},{33,1},{65,33},{97,65},{2,98}... | collective-permute-start | bytes 393224 | tf_op jit(solution)/shard_map/ppermute | solution.py:392
  85.2 3.7 %copy-start.5 = (f32[2,64,256]{2,1,0:T(8,128)}, f32[2,64,256]{2,1,0:T(8,128)S(1)}, u32[]{:S(2)}) copy-start(f32[2,64,256]{2,1,0:T(8,128)S(1)} %collective-permute-done.3.x1) | copy-start | bytes 393220
  87.5 1.4 %copy-start.6 = (f32[2,64,256]{2,1,0:T(8,128)}, f32[2,64,256]{2,1,0:T(8,128)S(1)}, u32[]{:S(2)}) copy-start(f32[2,64,256]{2,1,0:T(8,128)S(1)} %collective-permute-done.4.x2) | copy-start | bytes 393220
  88.9 0.7 copy-start.7
  88.9 0.8 copy-start.4
  91.7 7.2 %collective-permute-start.6 = (f32[64,256]{1,0:T(8,128)}, f32[64,256]{1,0:T(8,128)S(1)}, u32[]{:S(2)}, u32[]{:S(2)}) collective-permute-start(f32[64,256]{1,0:T(8,128)} %get-tuple-element.28), channel_id=1, source_target_pairs={{0,32},{32,64},{64,96},{96,0},{1,33},{33,65},{65,97},{97,1},{2,34}... | collective-permute-start | bytes 196616 | tf_op jit(solution)/shard_map/ppermute | solution.py:392
  92.2 6.6 %collective-permute-start.7 = (f32[64,256]{1,0:T(8,128)}, f32[64,256]{1,0:T(8,128)S(1)}, u32[]{:S(2)}, u32[]{:S(2)}) collective-permute-start(f32[64,256]{1,0:T(8,128)} %get-tuple-element.29), channel_id=1, source_target_pairs={{0,64},{32,96},{64,0},{96,32},{1,65},{33,97},{65,1},{97,33},{2,66}... | collective-permute-start | bytes 196616 | tf_op jit(solution)/shard_map/ppermute | solution.py:392
  95.2 4.5 %collective-permute-start.8 = (f32[64,256]{1,0:T(8,128)}, f32[64,256]{1,0:T(8,128)S(1)}, u32[]{:S(2)}, u32[]{:S(2)}) collective-permute-start(f32[64,256]{1,0:T(8,128)} %get-tuple-element.30), channel_id=1, source_target_pairs={{0,96},{32,0},{64,32},{96,64},{1,97},{33,1},{65,33},{97,65},{2,98}... | collective-permute-start | bytes 196616 | tf_op jit(solution)/shard_map/ppermute | solution.py:392
  97.2 4.5 %collective-permute-start.9 = (f32[64,256]{1,0:T(8,128)}, f32[64,256]{1,0:T(8,128)S(1)}, u32[]{:S(2)}, u32[]{:S(2)}) collective-permute-start(f32[64,256]{1,0:T(8,128)} %get-tuple-element.32), channel_id=1, source_target_pairs={{0,16},{16,0},{1,17},{17,1},{2,18},{18,2},{3,19},{19,3},{4,20},{20... | collective-permute-start | bytes 196616 | tf_op jit(solution)/shard_map/ppermute | solution.py:413
  98.8 2.9 %copy-start.8 = (f32[64,256]{1,0:T(8,128)}, f32[64,256]{1,0:T(8,128)S(1)}, u32[]{:S(2)}) copy-start(f32[64,256]{1,0:T(8,128)S(1)} %collective-permute-done.6.y1) | copy-start | bytes 196612
  98.8 2.9 %copy-start.9 = (f32[64,256]{1,0:T(8,128)}, f32[64,256]{1,0:T(8,128)S(1)}, u32[]{:S(2)}) copy-start(f32[64,256]{1,0:T(8,128)S(1)} %collective-permute-done.7.y2) | copy-start | bytes 196612
  99.7 2.1 %copy-start.10 = (f32[64,256]{1,0:T(8,128)}, f32[64,256]{1,0:T(8,128)S(1)}, u32[]{:S(2)}) copy-start(f32[64,256]{1,0:T(8,128)S(1)} %collective-permute-done.8.y3) | copy-start | bytes 196612
  101.7 0.6 copy-start.11
where the time goes:
time: 104 us
  Pallas kernels  41 us (39%)
  blocking collectives  32.1 us (31%)
  waiting for transfers between devices  13.9 us (13%)
  starting transfers between devices  11.2 us (11%)
  local copies, waits for them, and re-layouts  4.25 us (4%)
  other arithmetic  1.48 us (1%)
    pallas_call x1, Pallas kernels, projected_part(): pl.pallas_call(kernel, out_shape=[jax.ShapeDtypeStruct((size // BLK, BLK...  34.6 us
    all_to_all x1, blocking collectives, per_device(): lax.all_to_all(copies, CHIPS, split_axis=0, concat_axis=0, tiled=True)  32.1 us
    ppermute x6, starting transfers between devices, turned(): lax.ppermute(part, 'row_0', [(s, (s + k) % 4) for s in range(4)])  9.48 us
    ppermute x6, waiting for transfers between devices, turned(): lax.ppermute(part, 'row_0', [(s, (s + k) % 4) for s in range(4)])  7.17 us
    unnamed x27, local copies, waits for them, and re-layouts  3.44 us
    ppermute x1, waiting for transfers between devices, per_device(): other = lax.ppermute(mine, 'row_2', [(0, 1), (1, 0)])  2.85 us
    pallas_call x1, Pallas kernels, summed(): pl.pallas_call(pieces_first, out_shape=[shape(4), shape(4)] + [shape(2)]...  2.63 us
  transfers between devices with their start and end apart: 10, of which 7 were waited for; matrix products, arithmetic and copies ran while one was open for 1% of the time, Pallas kernels for 0%

commit v1 on v0

--- a/solution.py
+++ b/solution.py
@@ -38,32 +38,21 @@
     return jnp.broadcast_to(x[row : row + 1, :], (8, BLK))
 
 
-def factor_panels(rows, sub, lane):
+def factor_panels(rows, sub, lane, lines_ref):
     groups = len(rows)
-    late = []
-
-    def flush(chosen):
-        for g, update in [item for item in late if item[0] in chosen]:
-            update()
-        late[:] = [item for item in late if item[0] not in chosen]
-
     for t in range(0, groups, 2):
         first = 8 * t
-        flush((t, t + 1))
         pivot = [[], []]
         for m in range(16):
             for y in range(2):
                 pivot[y].append(lane_copy(rows[t + y], first + m))
-        below = {g: [] for g in range(t + 2, groups)}
-        near = [g for g in below if g < t + 4]
-        flush(near)
-        for m in range(16):
-            for g in near:
-                below[g].append(lane_copy(rows[g], first + m))
-        flush(range(groups))
-        for m in range(16):
-            for g in range(t + 4, groups):
-                below[g].append(lane_copy(rows[g], first + m))
+        near = range(t + 2, min(groups, t + 6))
+        far = range(t + 6, groups)
+        below = {g: [] for g in near}
+        for pair in range(0, len(near), 2):
+            for m in range(16):
+                for g in near[pair : pair + 2]:
+                    below[g].append(lane_copy(rows[g], first + m))
         here = (lane >= first) & (lane < first + 16)
         full = [
             jnp.where(here, jnp.where(lane - first - 8 * y == sub, 1.0, 0.0), rows[t + y])
@@ -112,35 +101,53 @@
                 low = row_copy(full[k // 8], k % 8 + 1)
                 lines += [qc * top - qb * low, qa * low - qb * top]
 
-            def update(g, lines=lines, below=below, here=here):
+            for g in near:
                 terms = [a * b for a, b in zip(below[g], lines)]
                 while len(terms) > 1:
                     terms = [a + b for a, b in zip(terms[::2], terms[1::2])]
                 rows[g] = jnp.where(here, 0.0, rows[g]) - terms[0]
-
-            for g in below:
-                if g in near:
-                    update(g)
-                else:
-                    late.append((g, lambda g=g, update=update: update(g)))
+        if far:
+            tall = []
+            for y in range(2):
+                value = lines[8 * y]
+                for i in range(1, 8):
+                    value = jnp.where(sub == i, lines[8 * y + i], value)
+                tall.append(value)
+            high, low = halves(jnp.concatenate(tall, axis=0))
+            for part, value in enumerate((high, high, low)):
+                lines_ref[t // 2, part * BLK + first : part * BLK + first + 16, :] = value
+            high, low = halves(jnp.concatenate([rows[g] for g in far], axis=0))
+            update = dot_bf16(jnp.concatenate([high, low, high], axis=1), lines_ref[t // 2])
+            for i, g in enumerate(far):
+                rows[g] = jnp.where(here, 0.0, rows[g]) - update[8 * i : 8 * i + 8]
         yield
+
+
+def at_ds(i):
+    return pl.ds(i * BLK, BLK)
 
 
 def kernel(
     where_ref, inv_mask, ks_mask, mine_ref, other_ref, coupling_hbm, lead_hbm, tail_hbm,
     kept_ref, sent_ref,
     m_ref, coupling_ref, lead_ref, tail_ref, ch_ref, cl_ref, kh_ref, kl_ref, th_ref, tl_ref,
-    before_ref, right_even, right_odd, left_ref, sem, strip_sem,
+    before_ref, right_even, right_odd, left_ref, lines_ref, last_ref, sem, strip_sem,
 ):
     right_refs = (right_even, right_odd)
     size = m_ref.shape[0]
     count = size // BLK
     row, col, core = where_ref[0], where_ref[1], where_ref[2]
-    copies = [
-        pltpu.make_async_copy(coupling_hbm, coupling_ref, sem.at[0]),
-        pltpu.make_async_copy(lead_hbm, lead_ref, sem.at[1]),
-        pltpu.make_async_copy(tail_hbm, tail_ref, sem.at[2]),
+    lead_copies = [
+        pltpu.make_async_copy(lead_hbm.at[at_ds(k), :], lead_ref.at[at_ds(k), :], sem.at[k])
+        for k in range(count)
     ]
+    coupling_copies = [
+        pltpu.make_async_copy(
+            coupling_hbm.at[at_ds(k), :], coupling_ref.at[at_ds(k), :], sem.at[count + k]
+        )
+        for k in range(count)
+    ]
+    tail_copy = pltpu.make_async_copy(tail_hbm, tail_ref, sem.at[2 * count])
     sub = lax.broadcasted_iota(jnp.int32, (8, BLK), 0)
     lane = lax.broadcasted_iota(jnp.int32, (8, BLK), 1)
 
@@ -173,8 +180,12 @@
     for b in range(count):
         for copy in strips[b]:
             copy.start()
-    for copy in copies:
-        copy.start()
+    tail_copy.start()
+    for k in range(count):
+        lead_copies[k].start()
+    for k in range(count):
+        coupling_copies[k].start()
+    lines_ref[...] = jnp.zeros(lines_ref.shape, BF16)
     for copy in strips[0]:
         copy.wait()
 
@@ -188,17 +199,25 @@
                 m_ref[at(c), at(b)] = m_ref[at(b), at(c)].T
             yield
 
+    def pause(steps):
+        for _ in range(steps):
+            yield
+
+    def split_coupling(k):
+        coupling_copies[k].wait()
+        for half in range(2):
+            wide = slice(half * size // 2, (half + 1) * size // 2)
+            ch_ref[at(k), wide], cl_ref[at(k), wide] = halves(coupling_ref[at(k), wide])
+            yield
+
     def prepare():
-        for copy in copies:
-            copy.wait()
         for k in range(count):
-            ch_ref[at(k), :], cl_ref[at(k), :] = halves(coupling_ref[at(k), :])
-            yield
-        for k in range(count):
+            lead_copies[k].wait()
             for n in range(lead_ref.shape[1] // BLK):
                 keep = ks_mask[row * count + k, col * 4 + n].astype(F32)
                 kh_ref[at(k), at(n)], kl_ref[at(k), at(n)] = halves(lead_ref[at(k), at(n)] * keep)
             yield
+        tail_copy.wait()
         th_ref[...] = jnp.zeros(th_ref.shape, BF16)
         tl_ref[...] = jnp.zeros(tl_ref.shape, BF16)
         lead_blocks = ks_mask.shape[0] - count
@@ -251,16 +270,32 @@
             eliminate(j, i, [part])
             yield
 
-    def project(i):
+    def early_lead():
+        coupling_copies[count - 1].wait()
+        depth = slice(0, size - BLK)
+        high, low = before_ref[0:BLK, depth], before_ref[2 * BLK :, depth]
+        for k in range(0, count, 2):
+            wide = slice(k * BLK, (k + 2) * BLK)
+            value = coupling_ref[size - BLK :, wide] + (
+                dot_bf16(high, ch_ref[depth, wide])
+                + (dot_bf16(high, cl_ref[depth, wide]) + dot_bf16(low, ch_ref[depth, wide]))
+            )
+            stack(last_ref, wide, value)
+            yield
+
+    def project(i, left):
         depth = slice(0, (i + 1) * BLK)
         right = right_refs[i % 2]
         high, low = right[0:BLK, depth], right[2 * BLK :, depth]
         total = None
         for k in range(0, count, 2):
             wide = slice(k * BLK, (k + 2) * BLK)
-            lead = dot_bf16(high, ch_ref[depth, wide]) + (
-                dot_bf16(high, cl_ref[depth, wide]) + dot_bf16(low, ch_ref[depth, wide])
-            )
+            if i + 1 == count:
+                lead = dot_bf16(left, last_ref[:, wide])
+            else:
+                lead = dot_bf16(high, ch_ref[depth, wide]) + (
+                    dot_bf16(high, cl_ref[depth, wide]) + dot_bf16(low, ch_ref[depth, wide])
+                )
             keep = [inv_mask[i, row * count + k + q].astype(F32) for q in range(2)]
             lead = jnp.concatenate([lead[:, :BLK] * keep[0], lead[:, BLK:] * keep[1]], axis=1)
             part = dot_three(lead, kh_ref[wide, :], kl_ref[wide, :])
@@ -275,11 +310,11 @@
         sent_ref[i] = jnp.where(core == 0, total[half:], total[:half])
         yield
 
-    fillers = [arrive(), prepare_row(0), prepare()]
+    fillers = [arrive(), prepare_row(0), pause(6), prepare(), split_coupling(0)]
     for j in range(count):
         rows = [m_ref[j * BLK + 8 * g : j * BLK + 8 * g + 8, at(j)] for g in range(16)]
-        for step in factor_panels(rows, sub, lane):
-            for _ in range(5):
+        for step in factor_panels(rows, sub, lane, lines_ref):
+            for _ in range(4):
                 while fillers:
                     try:
                         next(fillers[0])
@@ -310,7 +345,11 @@
         fillers = []
         if j + 1 < count:
             fillers += [trailing(j, j + 1, True), prepare_row(j + 1)]
-        fillers += [trailing(j, i, False) for i in range(j + 2, count)] + [project(j)]
+            if j + 2 < count:
+                fillers.append(split_coupling(j + 1))
+            else:
+                fillers.append(early_lead())
+        fillers += [trailing(j, i, False) for i in range(j + 2, count)] + [project(j, left)]
     while fillers:
         for _ in fillers.pop(0):
             pass
@@ -342,16 +381,18 @@
             pltpu.VMEM((3 * BLK, size), BF16),
             pltpu.VMEM((3 * BLK, size), BF16),
             pltpu.VMEM((size // BLK, BLK, 3 * BLK), BF16),
-            pltpu.SemaphoreType.DMA((3,)),
+            pltpu.VMEM((5, 3 * BLK, BLK), BF16),
+            pltpu.VMEM((3 * BLK, size), BF16),
+            pltpu.SemaphoreType.DMA((17,)),
             pltpu.SemaphoreType.DMA((28,)),
         ],
-        compiler_params=pltpu.CompilerParams(vmem_limit_bytes=48 * 1024 * 1024),
+        compiler_params=pltpu.CompilerParams(vmem_limit_bytes=36 * 1024 * 1024),
         name="project",
     )(place, inv_mask, ks_mask, mine, other, coupling, ks_lead, ks_tail)
 
 
 def pieces_first(where_ref, kept, got, z_kept, z_sent, x_own, *x_sent):
-    x, z = where_ref[0], where_ref[1]
+    x, z = where_ref[3], where_ref[4]
     half = kept.shape[-1] // 2
     lo, hi = slice(0, half), slice(half, 2 * half)
     for i in range(4):
@@ -364,7 +405,7 @@
 
 
 def pieces_second(where_ref, z_kept, z_got, x_own, x1, x2, x3, y_own, y1, y2, y3, v_kept, v_sent):
-    x, z = where_ref[0], where_ref[1]
+    x, z = where_ref[3], where_ref[4]
     for k, ref in enumerate((y_own, y1, y2, y3)):
         to = lax.rem(x + k, 4)
         ref[...] = z_kept[to] + z_got[to]
@@ -399,6 +440,7 @@
         out_shape=[shape(4), shape(4)] + [shape(2)] * 4,
         in_specs=[smem, vmem, vmem],
         out_specs=[vmem] * 6,
+        compiler_params=pltpu.CompilerParams(vmem_limit_bytes=4 * 1024 * 1024),
         name="pieces_first",
     )(where, kept, got)
     z_got = lax.ppermute(z_sent, "row_1", swap)
@@ -408,6 +450,7 @@
         out_shape=[shape()] * 6,
         in_specs=[smem] + [vmem] * 6,
         out_specs=[vmem] * 6,
+        compiler_params=pltpu.CompilerParams(vmem_limit_bytes=4 * 1024 * 1024),
         name="pieces_second",
     )(where, z_kept, z_got, x_own, *x_got)
     v_got = lax.ppermute(v_sent, "row_1", swap)
@@ -417,6 +460,7 @@
         out_shape=jax.ShapeDtypeStruct((rows, 2 * half), F32),
         in_specs=[vmem] * 6,
         out_specs=vmem,
+        compiler_params=pltpu.CompilerParams(vmem_limit_bytes=4 * 1024 * 1024),
         name="pieces_third",
     )(y_own, *y_got, v_kept, v_got)
 
@@ -434,10 +478,11 @@
     mine = lax.all_to_all(copies, CHIPS, split_axis=0, concat_axis=0, tiled=True)
     mine = mine.reshape(-1, BLK // 2, SENT * BLK)
     other = lax.ppermute(mine, "row_2", [(0, 1), (1, 0)])
-    place = jnp.stack([row_index, col_index, core_index]).astype(jnp.int32)
+    place = jnp.stack(
+        [row_index, col_index, core_index, lax.axis_index("row_0"), lax.axis_index("row_1")]
+    ).astype(jnp.int32)
     kept, sent = projected_part(place, inv_mask, ks_mask, mine, other, coupling, ks_lead, ks_tail)
-    where = jnp.stack([lax.axis_index("row_0"), lax.axis_index("row_1")]).astype(jnp.int32)
-    return summed(where, kept, sent)
+    return summed(place, kept, sent)
 
 
 def solution(mesh):

time: 104 us -> 99.8 us (0.960)
  Pallas kernels: 41 us -> 36.7 us
    pallas_call x1, Pallas kernels: 2.63 us -> 0.68 us  [summed(): pl.pallas_call(pieces_first, out_shape=[shape(4), shape(4)] + [shape(2)]...]
    pallas_call x1, Pallas kernels: 2.02 us -> 0.6 us  [summed(): pl.pallas_call(pieces_second, out_shape=[shape()] * 6, in_specs=[smem] +...]
    unnamed x27 -> x11, local copies, waits for them, and re-layouts: 3.44 us -> 3.21 us
  transfers between devices with their start and end apart: 10 -> 10, of which waited for: 7 -> 7; matrix products, arithmetic and copies ran while one was open for 1% -> 0% of each run, Pallas kernels for 0% -> 0%
where the time goes in v1:
time: 99.8 us; the launch traced here: 99.5 us
  Pallas kernels  36.7 us (37%)
  blocking collectives  32.1 us (32%)
  waiting for transfers between devices  14.3 us (14%)
  starting transfers between devices  11.4 us (11%)
  local copies, waits for them, and re-layouts  4.1 us (4%)
    pallas_call x1, Pallas kernels, projected_part(): pl.pallas_call(kernel, out_shape=[jax.ShapeDtypeStruct((size // BLK, BLK...  34.8 us
    all_to_all x1, blocking collectives, per_device(): lax.all_to_all(copies, CHIPS, split_axis=0, concat_axis=0, tiled=True)  32.1 us
    ppermute x6, starting transfers between devices, turned(): lax.ppermute(part, 'row_0', [(s, (s + k) % 4) for s in range(4)])  9.6 us
    ppermute x6, waiting for transfers between devices, turned(): lax.ppermute(part, 'row_0', [(s, (s + k) % 4) for s in range(4)])  6.87 us
    unnamed x11, local copies, waits for them, and re-layouts  3.21 us
    ppermute x1, waiting for transfers between devices, per_device(): other = lax.ppermute(mine, 'row_2', [(0, 1), (1, 0)])  2.97 us
    ppermute x1, waiting for transfers between devices, summed(): got = lax.ppermute(sent, 'row_2', swap)  2.53 us
  transfers between devices with their start and end apart: 10, of which 7 were waited for; matrix products, arithmetic and copies ran while one was open for 0% of the time, Pallas kernels for 0%

profile of v1, /device:TPU:2, one launch (start us, length us, event | category | flops | bytes accessed | tf_op | source)
XLA Modules:
  0.0 99.5 jit_solution(16769295695415601053)
XLA Ops:
  0.0 0.7 slice.3
  0.7 0.7 fusion
  1.5 0.1 broadcast_in_dim.2
  1.6 0.0 copy-start.4
  1.6 0.0 copy-start.1
  1.6 0.0 copy-start.3
  1.6 32.1 %all_to_all.5 = f32[64,8,640]{2,1,0:T(8,128)S(1)} all-to-all(f32[64,8,640]{2,1,0:T(8,128)S(1)} %broadcast_in_dim.2), channel_id=1, replica_groups=mesh['row_0'=4,'row_1'=2,'row_2'=2,'col_0'=4,'col_1'=2] {'row_0','row_1'..., dimensions={0} | all-to-all | bytes 2621440 | tf_op jit(solution)/shard_map/all_to_all | solution.py:478
  33.7 0.0 collective-permute-start
  33.7 0.0 copy-done.4
  33.7 0.1 copy.7.ks_mask
  33.8 0.1 stack.23.where_ref
  33.9 3.0 %collective-permute-done.other_ref = f32[8,64,640]{2,1,0:T(8,128)} collective-permute-done((f32[8,64,640]{2,1,0:T(8,128)S(1)}, f32[8,64,640]{2,1,0:T(8,128)}, u32[]{:S(2)}, u32[]{:S(2)}) %collective-permute-start) | collective-permute-done | bytes 1310752 | tf_op jit(solution)/shard_map/ppermute | solution.py:480
  36.8 0.0 copy-done.1
  36.8 0.0 copy-done.3
  36.8 0.0 copy-start
  36.8 2.2 %copy-done = f32[1024,1024]{1,0:T(8,128)S(1)} copy-done((f32[1024,1024]{1,0:T(8,128)S(1)}, f32[1024,1024]{1,0:T(8,128)}, u32[]{:S(2)}) %copy-start) | copy-done | bytes 4194328
  39.0 0.0 copy-start.2
  39.0 0.9 copy-done.2
  39.9 34.8 %project.1 = (f32[8,64,512]{2,1,0:T(8,128)S(1)}, f32[8,64,512]{2,1,0:T(8,128)S(1)}) custom-call(s32[5]{0:T(128)S(1)} %stack.23.where_ref, s32[8,136]{1,0:T(8,128)S(1)} %copy-done.3, s32[136,32]{1,0:T(8,128)S(1)} %copy.7.ks_mask, f32[8,64,640]{2,1,0:T(8,128)S(1)} %bitcast.7, f32[8,64,640]{2,1,0:T(8,128)} %collective-permute-done.other_ref, ...), custom_call_target="tpu_custom_call" | custom-call | tf_op jit(solution)/shard_map/project/pallas_call | solution.py:364
  74.7 0.2 collective-permute-start.1
  74.9 2.5 %collective-permute-done.1.got = f32[8,64,512]{2,1,0:T(8,128)S(1)} collective-permute-done((f32[8,64,512]{2,1,0:T(8,128)S(1)}, f32[8,64,512]{2,1,0:T(8,128)S(1)}, u32[]{:S(2)}, u32[]{:S(2)}) %collective-permute-start.1) | collective-permute-done | bytes 1048608 | tf_op jit(solution)/shard_map/ppermute | solution.py:437
  77.5 0.7 pieces_first.1
  78.1 0.1 collective-permute-start.2
  78.2 0.8 collective-permute-start.3
  79.0 2.7 %collective-permute-start.4 = (f32[2,64,256]{2,1,0:T(8,128)S(1)}, f32[2,64,256]{2,1,0:T(8,128)S(1)}, u32[]{:S(2)}, u32[]{:S(2)}) collective-permute-start(f32[2,64,256]{2,1,0:T(8,128)S(1)} %get-tuple-element.25), channel_id=1, source_target_pairs={{0,64},{32,96},{64,0},{96,32},{1,65},{33,97},{65,1},{97,33},{2,66}... | collective-permute-start | bytes 393224 | tf_op jit(solution)/shard_map/ppermute | solution.py:433
  81.7 0.5 collective-permute-start.5
  82.2 2.5 %collective-permute-done.3.x1 = f32[2,64,256]{2,1,0:T(8,128)S(1)} collective-permute-done((f32[2,64,256]{2,1,0:T(8,128)S(1)}, f32[2,64,256]{2,1,0:T(8,128)S(1)}, u32[]{:S(2)}, u32[]{:S(2)}) %collective-permute-start.3) | collective-permute-done | bytes 131104 | tf_op jit(solution)/shard_map/ppermute | solution.py:433
  84.7 2.2 %collective-permute-done.4.x2 = f32[2,64,256]{2,1,0:T(8,128)S(1)} collective-permute-done((f32[2,64,256]{2,1,0:T(8,128)S(1)}, f32[2,64,256]{2,1,0:T(8,128)S(1)}, u32[]{:S(2)}, u32[]{:S(2)}) %collective-permute-start.4) | collective-permute-done | bytes 131104 | tf_op jit(solution)/shard_map/ppermute | solution.py:433
  86.9 1.4 %collective-permute-done.5.x3 = f32[2,64,256]{2,1,0:T(8,128)S(1)} collective-permute-done((f32[2,64,256]{2,1,0:T(8,128)S(1)}, f32[2,64,256]{2,1,0:T(8,128)S(1)}, u32[]{:S(2)}, u32[]{:S(2)}) %collective-permute-start.5) | collective-permute-done | bytes 131104 | tf_op jit(solution)/shard_map/ppermute | solution.py:433
  88.3 0.0 collective-permute-done.2.z_got
  88.3 0.6 pieces_second.1
  88.9 0.6 collective-permute-start.6
  89.5 3.1 %collective-permute-start.7 = (f32[64,256]{1,0:T(8,128)S(1)}, f32[64,256]{1,0:T(8,128)S(1)}, u32[]{:S(2)}, u32[]{:S(2)}) collective-permute-start(f32[64,256]{1,0:T(8,128)S(1)} %get-tuple-element.29), channel_id=1, source_target_pairs={{0,64},{32,96},{64,0},{96,32},{1,65},{33,97},{65,1},{97,33},{2,66}... | collective-permute-start | bytes 196616 | tf_op jit(solution)/shard_map/ppermute | solution.py:433
  92.6 2.0 %collective-permute-start.8 = (f32[64,256]{1,0:T(8,128)S(1)}, f32[64,256]{1,0:T(8,128)S(1)}, u32[]{:S(2)}, u32[]{:S(2)}) collective-permute-start(f32[64,256]{1,0:T(8,128)S(1)} %get-tuple-element.30), channel_id=1, source_target_pairs={{0,96},{32,0},{64,32},{96,64},{1,97},{33,1},{65,33},{97,65},{2,98}... | collective-permute-start | bytes 196616 | tf_op jit(solution)/shard_map/ppermute | solution.py:433
  94.6 1.5 %collective-permute-start.9 = (f32[64,256]{1,0:T(8,128)S(1)}, f32[64,256]{1,0:T(8,128)S(1)}, u32[]{:S(2)}, u32[]{:S(2)}) collective-permute-start(f32[64,256]{1,0:T(8,128)S(1)} %get-tuple-element.32), channel_id=1, source_target_pairs={{0,16},{16,0},{1,17},{17,1},{2,18},{18,2},{3,19},{19,3},{4,20},{20... | collective-permute-start | bytes 196616 | tf_op jit(solution)/shard_map/ppermute | solution.py:456
  96.1 0.0 collective-permute-done.6.y1
  96.1 0.0 collective-permute-done.7.y2
  96.1 0.8 collective-permute-done.8.y3
  96.9 2.0 %collective-permute-done.9.v_got = f32[64,256]{1,0:T(8,128)S(1)} collective-permute-done((f32[64,256]{1,0:T(8,128)S(1)}, f32[64,256]{1,0:T(8,128)S(1)}, u32[]{:S(2)}, u32[]{:S(2)}) %collective-permute-start.9) | collective-permute-done | bytes 65568 | tf_op jit(solution)/shard_map/ppermute | solution.py:456
  98.8 0.7 pieces_third.1
Async XLA Ops:
  1.6 32.1 %copy-start.4 = (s32[136,32]{0,1:T(8,128)S(1)}, s32[136,32]{0,1:T(8,128)}, u32[]{:S(2)}) copy-start(s32[136,32]{0,1:T(8,128)} %param.11) | copy-start | bytes 52228
  1.6 35.3 %copy-start.1 = (f32[1024,512]{1,0:T(8,128)S(1)}, f32[1024,512]{1,0:T(8,128)}, u32[]{:S(2)}) copy-start(f32[1024,512]{1,0:T(8,128)} %lead_hbm.1) | copy-start | bytes 6291460
  1.6 35.3 %copy-start.3 = (s32[8,136]{1,0:T(8,128)S(1)}, s32[8,136]{1,0:T(8,128)}, u32[]{:S(2)}) copy-start(s32[8,136]{1,0:T(8,128)} %inv_mask.1) | copy-start | bytes 13060
  33.7 3.2 %collective-permute-start = (f32[8,64,640]{2,1,0:T(8,128)S(1)}, f32[8,64,640]{2,1,0:T(8,128)}, u32[]{:S(2)}, u32[]{:S(2)}) collective-permute-start(f32[8,64,640]{2,1,0:T(8,128)S(1)} %bitcast.6), channel_id=1, source_target_pairs={{0,8},{8,0},{1,9},{9,1},{2,10},{10,2},{3,11},{11,3},{4,12},{12,4},... | collective-permute-start | bytes 3932168 | tf_op jit(solution)/shard_map/ppermute | solution.py:480
  36.8 2.2 %copy-start = (f32[1024,1024]{1,0:T(8,128)S(1)}, f32[1024,1024]{1,0:T(8,128)}, u32[]{:S(2)}) copy-start(f32[1024,1024]{1,0:T(8,128)} %coupling_hbm.1) | copy-start | bytes 12582916
  39.0 0.9 copy-start.2
  74.7 2.7 %collective-permute-start.1 = (f32[8,64,512]{2,1,0:T(8,128)S(1)}, f32[8,64,512]{2,1,0:T(8,128)S(1)}, u32[]{:S(2)}, u32[]{:S(2)}) collective-permute-start(f32[8,64,512]{2,1,0:T(8,128)S(1)} %get-tuple-element.20), channel_id=1, source_target_pairs={{0,8},{8,0},{1,9},{9,1},{2,10},{10,2},{3,11},{11,3},{4,12},{12,4},... | collective-permute-start | bytes 3145736 | tf_op jit(solution)/shard_map/ppermute | solution.py:437
  78.1 10.1 %collective-permute-start.2 = (f32[4,64,256]{2,1,0:T(8,128)S(1)}, f32[4,64,256]{2,1,0:T(8,128)S(1)}, u32[]{:S(2)}, u32[]{:S(2)}) collective-permute-start(f32[4,64,256]{2,1,0:T(8,128)S(1)} %get-tuple-element.22), channel_id=1, source_target_pairs={{0,16},{16,0},{1,17},{17,1},{2,18},{18,2},{3,19},{19,3},{4,20},{20... | collective-permute-start | bytes 786440 | tf_op jit(solution)/shard_map/ppermute | solution.py:446
  78.2 6.4 %collective-permute-start.3 = (f32[2,64,256]{2,1,0:T(8,128)S(1)}, f32[2,64,256]{2,1,0:T(8,128)S(1)}, u32[]{:S(2)}, u32[]{:S(2)}) collective-permute-start(f32[2,64,256]{2,1,0:T(8,128)S(1)} %get-tuple-element.24), channel_id=1, source_target_pairs={{0,32},{32,64},{64,96},{96,0},{1,33},{33,65},{65,97},{97,1},{2,34}... | collective-permute-start | bytes 393224 | tf_op jit(solution)/shard_map/ppermute | solution.py:433
  79.0 7.9 %collective-permute-start.4 = (f32[2,64,256]{2,1,0:T(8,128)S(1)}, f32[2,64,256]{2,1,0:T(8,128)S(1)}, u32[]{:S(2)}, u32[]{:S(2)}) collective-permute-start(f32[2,64,256]{2,1,0:T(8,128)S(1)} %get-tuple-element.25), channel_id=1, source_target_pairs={{0,64},{32,96},{64,0},{96,32},{1,65},{33,97},{65,1},{97,33},{2,66}... | collective-permute-start | bytes 393224 | tf_op jit(solution)/shard_map/ppermute | solution.py:433
  81.7 6.6 %collective-permute-start.5 = (f32[2,64,256]{2,1,0:T(8,128)S(1)}, f32[2,64,256]{2,1,0:T(8,128)S(1)}, u32[]{:S(2)}, u32[]{:S(2)}) collective-permute-start(f32[2,64,256]{2,1,0:T(8,128)S(1)} %get-tuple-element.26), channel_id=1, source_target_pairs={{0,96},{32,0},{64,32},{96,64},{1,97},{33,1},{65,33},{97,65},{2,98}... | collective-permute-start | bytes 393224 | tf_op jit(solution)/shard_map/ppermute | solution.py:433
  88.9 7.2 %collective-permute-start.6 = (f32[64,256]{1,0:T(8,128)S(1)}, f32[64,256]{1,0:T(8,128)S(1)}, u32[]{:S(2)}, u32[]{:S(2)}) collective-permute-start(f32[64,256]{1,0:T(8,128)S(1)} %get-tuple-element.28), channel_id=1, source_target_pairs={{0,32},{32,64},{64,96},{96,0},{1,33},{33,65},{65,97},{97,1},{2,34}... | collective-permute-start | bytes 196616 | tf_op jit(solution)/shard_map/ppermute | solution.py:433
  89.5 6.6 %collective-permute-start.7 = (f32[64,256]{1,0:T(8,128)S(1)}, f32[64,256]{1,0:T(8,128)S(1)}, u32[]{:S(2)}, u32[]{:S(2)}) collective-permute-start(f32[64,256]{1,0:T(8,128)S(1)} %get-tuple-element.29), channel_id=1, source_target_pairs={{0,64},{32,96},{64,0},{96,32},{1,65},{33,97},{65,1},{97,33},{2,66}... | collective-permute-start | bytes 196616 | tf_op jit(solution)/shard_map/ppermute | solution.py:433
  92.6 4.3 %collective-permute-start.8 = (f32[64,256]{1,0:T(8,128)S(1)}, f32[64,256]{1,0:T(8,128)S(1)}, u32[]{:S(2)}, u32[]{:S(2)}) collective-permute-start(f32[64,256]{1,0:T(8,128)S(1)} %get-tuple-element.30), channel_id=1, source_target_pairs={{0,96},{32,0},{64,32},{96,64},{1,97},{33,1},{65,33},{97,65},{2,98}... | collective-permute-start | bytes 196616 | tf_op jit(solution)/shard_map/ppermute | solution.py:433
  94.6 4.3 %collective-permute-start.9 = (f32[64,256]{1,0:T(8,128)S(1)}, f32[64,256]{1,0:T(8,128)S(1)}, u32[]{:S(2)}, u32[]{:S(2)}) collective-permute-start(f32[64,256]{1,0:T(8,128)S(1)} %get-tuple-element.32), channel_id=1, source_target_pairs={{0,16},{16,0},{1,17},{17,1},{2,18},{18,2},{3,19},{19,3},{4,20},{20... | collective-permute-start | bytes 196616 | tf_op jit(solution)/shard_map/ppermute | solution.py:456

commit v2 on v1

--- a/solution.py
+++ b/solution.py
@@ -23,11 +23,6 @@
 def halves(x):
     high = x.astype(BF16)
     return high, (x - high.astype(F32)).astype(BF16)
-
-
-def dot_three(a, b_high, b_low):
-    high, low = halves(a)
-    return dot_bf16(high, b_high) + (dot_bf16(high, b_low) + dot_bf16(low, b_high))
 
 
 def lane_copy(x, column):
@@ -76,13 +71,18 @@
                     others = (sub < i) | (sub > i + 1)
                     u, v = jnp.where(others, u, 0.0), jnp.where(others, v, 0.0)
                 left.append((u, v))
-            for m in range(k + 2, 16):
+            for m in range(k + 2, min(k + 4, 16)):
                 top, low = row_copy(pivot[x][m], i), row_copy(pivot[x][m], i + 1)
                 for y in range(2):
                     pivot[y][m] = pivot[y][m] - (left[y][0] * top + left[y][1] * low) * q
+            left = [(u * q, v * q) for u, v in left]
+            for m in range(k + 4, 16):
+                top, low = row_copy(pivot[x][m], i), row_copy(pivot[x][m], i + 1)
+                for y in range(2):
+                    pivot[y][m] = pivot[y][m] - (left[y][0] * top + left[y][1] * low)
             top, low = row_copy(full[x], i), row_copy(full[x], i + 1)
             for y in range(2):
-                full[y] = full[y] - (left[y][0] * top + left[y][1] * low) * q
+                full[y] = full[y] - (left[y][0] * top + left[y][1] * low)
             root_a = lax.rsqrt(a)
             over_a = root_a * root_a
             root_c = lax.rsqrt(det * over_a)
@@ -130,7 +130,7 @@
 def kernel(
     where_ref, inv_mask, ks_mask, mine_ref, other_ref, coupling_hbm, lead_hbm, tail_hbm,
     kept_ref, sent_ref,
-    m_ref, coupling_ref, lead_ref, tail_ref, ch_ref, cl_ref, kh_ref, kl_ref, th_ref, tl_ref,
+    m_ref, coupling_ref, lead_ref, tail_ref, c_ref, k_ref, t_ref, x_ref, lead_stack,
     before_ref, right_even, right_odd, left_ref, lines_ref, last_ref, sem, strip_sem,
 ):
     right_refs = (right_even, right_odd)
@@ -207,7 +207,9 @@
         coupling_copies[k].wait()
         for half in range(2):
             wide = slice(half * size // 2, (half + 1) * size // 2)
-            ch_ref[at(k), wide], cl_ref[at(k), wide] = halves(coupling_ref[at(k), wide])
+            high, low = halves(coupling_ref[at(k), wide])
+            for part, value in enumerate((high, high, low)):
+                c_ref[at(3 * k + part), wide] = value
             yield
 
     def prepare():
@@ -215,17 +217,18 @@
             lead_copies[k].wait()
             for n in range(lead_ref.shape[1] // BLK):
                 keep = ks_mask[row * count + k, col * 4 + n].astype(F32)
-                kh_ref[at(k), at(n)], kl_ref[at(k), at(n)] = halves(lead_ref[at(k), at(n)] * keep)
+                high, low = halves(lead_ref[at(k), at(n)] * keep)
+                for part, value in enumerate((high, high, low)):
+                    k_ref[at(3 * k + part), at(n)] = value
             yield
         tail_copy.wait()
-        th_ref[...] = jnp.zeros(th_ref.shape, BF16)
-        tl_ref[...] = jnp.zeros(tl_ref.shape, BF16)
+        t_ref[...] = jnp.zeros(t_ref.shape, BF16)
         lead_blocks = ks_mask.shape[0] - count
         for n in range(lead_ref.shape[1] // BLK):
             keep = ks_mask[lead_blocks + row // 2, col * 4 + n].astype(F32)
             high, low = halves(tail_ref[:, at(n)] * keep)
-            th_ref[pl.ds(core * 64, 64), at(n)] = high
-            tl_ref[pl.ds(core * 64, 64), at(n)] = low
+            for part, value in enumerate((high, high, low)):
+                t_ref[pl.ds(pl.multiple_of(part * BLK + core * 64, 64), 64), at(n)] = value
         yield
 
     def stack(ref, cols, value):
@@ -270,45 +273,50 @@
             eliminate(j, i, [part])
             yield
 
+    def beside_into(ref, block, value):
+        high, low = halves(value)
+        for part, piece in enumerate((high, low, high)):
+            ref[:, at(3 * block + part)] = piece
+
     def early_lead():
         coupling_copies[count - 1].wait()
-        depth = slice(0, size - BLK)
-        high, low = before_ref[0:BLK, depth], before_ref[2 * BLK :, depth]
+        for k in range(count - 1):
+            beside_into(x_ref, k, m_ref[at(count - 1), at(k)])
+        yield
+        depth = slice(0, 3 * (size - BLK))
         for k in range(0, count, 2):
             wide = slice(k * BLK, (k + 2) * BLK)
-            value = coupling_ref[size - BLK :, wide] + (
-                dot_bf16(high, ch_ref[depth, wide])
-                + (dot_bf16(high, cl_ref[depth, wide]) + dot_bf16(low, ch_ref[depth, wide]))
-            )
+            value = coupling_ref[size - BLK :, wide] + dot_bf16(x_ref[:, depth], c_ref[depth, wide])
             stack(last_ref, wide, value)
             yield
 
     def project(i, left):
-        depth = slice(0, (i + 1) * BLK)
-        right = right_refs[i % 2]
-        high, low = right[0:BLK, depth], right[2 * BLK :, depth]
-        total = None
+        depth = slice(0, 3 * (i + 1) * BLK)
+        if i + 1 < count:
+            for k in range(i):
+                beside_into(x_ref, k, m_ref[at(i), at(k)])
+            x_ref[:, 3 * i * BLK : 3 * (i + 1) * BLK] = left
+            yield
         for k in range(0, count, 2):
             wide = slice(k * BLK, (k + 2) * BLK)
             if i + 1 == count:
                 lead = dot_bf16(left, last_ref[:, wide])
             else:
-                lead = dot_bf16(high, ch_ref[depth, wide]) + (
-                    dot_bf16(high, cl_ref[depth, wide]) + dot_bf16(low, ch_ref[depth, wide])
-                )
-            keep = [inv_mask[i, row * count + k + q].astype(F32) for q in range(2)]
-            lead = jnp.concatenate([lead[:, :BLK] * keep[0], lead[:, BLK:] * keep[1]], axis=1)
-            part = dot_three(lead, kh_ref[wide, :], kl_ref[wide, :])
-            total = part if total is None else total + part
+                lead = dot_bf16(x_ref[:, depth], c_ref[depth, wide])
+            for q in range(2):
+                keep = inv_mask[i, row * count + k + q].astype(F32)
+                beside_into(lead_stack, k + q, lead[:, q * BLK : (q + 1) * BLK] * keep)
             yield
         mine = m_ref[at(i), pl.ds(pl.multiple_of(row // 2 * BLK, BLK), BLK)]
         keep = inv_mask[i, inv_mask.shape[1] - count + row // 2]
-        mine = jnp.where((keep != 0) & (row // 2 <= i), mine, 0.0)
-        total = dot_three(mine, th_ref[...], tl_ref[...]) - total
+        mine = beside(jnp.where((keep != 0) & (row // 2 <= i), mine, 0.0))
         half = BLK // 2
-        kept_ref[i] = jnp.where(core == 0, total[:half], total[half:])
-        sent_ref[i] = jnp.where(core == 0, total[half:], total[:half])
-        yield
+        for n in range(0, k_ref.shape[1], 2 * BLK):
+            wide = slice(n, n + 2 * BLK)
+            total = dot_bf16(mine, t_ref[:, wide]) - dot_bf16(lead_stack[...], k_ref[:, wide])
+            kept_ref[i, :, wide] = jnp.where(core == 0, total[:half], total[half:])
+            sent_ref[i, :, wide] = jnp.where(core == 0, total[half:], total[:half])
+            yield
 
     fillers = [arrive(), prepare_row(0), pause(6), prepare(), split_coupling(0)]
     for j in range(count):
@@ -371,12 +379,11 @@
             pltpu.VMEM(coupling.shape, F32),
             pltpu.VMEM(ks_lead.shape, F32),
             pltpu.VMEM(ks_tail.shape, F32),
-            pltpu.VMEM(coupling.shape, BF16),
-            pltpu.VMEM(coupling.shape, BF16),
-            pltpu.VMEM(ks_lead.shape, BF16),
-            pltpu.VMEM(ks_lead.shape, BF16),
-            pltpu.VMEM((BLK, width), BF16),
-            pltpu.VMEM((BLK, width), BF16),
+            pltpu.VMEM((3 * size, coupling.shape[1]), BF16),
+            pltpu.VMEM((3 * lead, width), BF16),
+            pltpu.VMEM((3 * BLK, width), BF16),
+            pltpu.VMEM((BLK, 3 * size), BF16),
+            pltpu.VMEM((BLK, 3 * lead), BF16),
             pltpu.VMEM((3 * BLK, size), BF16),
             pltpu.VMEM((3 * BLK, size), BF16),
             pltpu.VMEM((3 * BLK, size), BF16),
@@ -386,7 +393,7 @@
             pltpu.SemaphoreType.DMA((17,)),
             pltpu.SemaphoreType.DMA((28,)),
         ],
-        compiler_params=pltpu.CompilerParams(vmem_limit_bytes=36 * 1024 * 1024),
+        compiler_params=pltpu.CompilerParams(vmem_limit_bytes=48 * 1024 * 1024),
         name="project",
     )(place, inv_mask, ks_mask, mine, other, coupling, ks_lead, ks_tail)
 

time: 99.8 us -> 93.7 us (0.939)
  local copies, waits for them, and re-layouts: 4.1 us -> 1.01 us
  Pallas kernels: 36.7 us -> 33.9 us
    unnamed x11 -> x7, local copies, waits for them, and re-layouts: 3.21 us -> 0.12 us
    pallas_call x1, Pallas kernels: 34.8 us -> 31.9 us  [projected_part(): pl.pallas_call(kernel, out_shape=[jax.ShapeDtypeStruct((size // BLK, BLK...]
where the time goes in v2:
time: 93.7 us; the launch traced here: 93.4 us
  Pallas kernels  33.9 us (36%)
  blocking collectives  32.1 us (34%)
  waiting for transfers between devices  14.2 us (15%)
  starting transfers between devices  11.5 us (12%)
  local copies, waits for them, and re-layouts  1.01 us (1%)
    all_to_all x1, blocking collectives, per_device(): lax.all_to_all(copies, CHIPS, split_axis=0, concat_axis=0, tiled=True)  32.1 us
    pallas_call x1, Pallas kernels, projected_part(): pl.pallas_call(kernel, out_shape=[jax.ShapeDtypeStruct((size // BLK, BLK...  31.9 us
    ppermute x6, starting transfers between devices, turned(): lax.ppermute(part, 'row_0', [(s, (s + k) % 4) for s in range(4)])  9.6 us
    ppermute x6, waiting for transfers between devices, turned(): lax.ppermute(part, 'row_0', [(s, (s + k) % 4) for s in range(4)])  6.84 us
    ppermute x1, waiting for transfers between devices, per_device(): other = lax.ppermute(mine, 'row_2', [(0, 1), (1, 0)])  2.84 us
    ppermute x1, waiting for transfers between devices, summed(): got = lax.ppermute(sent, 'row_2', swap)  2.52 us
    ppermute x1, waiting for transfers between devices, summed(): v_got = lax.ppermute(v_sent, 'row_1', swap)  1.97 us
  transfers between devices with their start and end apart: 10, of which 7 were waited for; matrix products, arithmetic and copies ran while one was open for 0% of the time, Pallas kernels for 0%

profile of v2, /device:TPU:2, one launch (start us, length us, event | category | flops | bytes accessed | tf_op | source)
XLA Modules:
  0.0 93.4 jit_solution(16576286274013571277)
XLA Ops:
  0.0 0.7 slice.3
  0.7 0.7 fusion
  1.5 0.1 broadcast_in_dim.2
  1.6 0.0 copy-start.2
  1.6 0.0 copy-start
  1.6 0.0 copy-start.1
  1.6 32.1 %all_to_all.5 = f32[64,8,640]{2,1,0:T(8,128)S(1)} all-to-all(f32[64,8,640]{2,1,0:T(8,128)S(1)} %broadcast_in_dim.2), channel_id=1, replica_groups=mesh['row_0'=4,'row_1'=2,'row_2'=2,'col_0'=4,'col_1'=2] {'row_0','row_1'..., dimensions={0} | all-to-all | bytes 2621440 | tf_op jit(solution)/shard_map/all_to_all | solution.py:485
  33.7 0.0 collective-permute-start
  33.7 0.0 copy-done.2
  33.7 0.1 copy.7.ks_mask
  33.8 0.1 stack.23.where_ref
  33.9 2.8 %collective-permute-done.other_ref = f32[8,64,640]{2,1,0:T(8,128)S(1)} collective-permute-done((f32[8,64,640]{2,1,0:T(8,128)S(1)}, f32[8,64,640]{2,1,0:T(8,128)S(1)}, u32[]{:S(2)}, u32[]{:S(2)}) %collective-permute-start) | collective-permute-done | bytes 1310752 | tf_op jit(solution)/shard_map/ppermute | solution.py:487
  36.7 0.0 copy-done
  36.7 0.0 copy-done.1
  36.7 31.9 %project.1 = (f32[8,64,512]{2,1,0:T(8,128)S(1)}, f32[8,64,512]{2,1,0:T(8,128)S(1)}) custom-call(s32[5]{0:T(128)S(1)} %stack.23.where_ref, s32[8,136]{1,0:T(8,128)S(1)} %copy-done.1, s32[136,32]{1,0:T(8,128)S(1)} %copy.7.ks_mask, f32[8,64,640]{2,1,0:T(8,128)S(1)} %bitcast.7, f32[8,64,640]{2,1,0:T(8,128)S(1)} %collective-permute-done.other_ref, ...), custom_call_target="tpu_custom_call" | custom-call | tf_op jit(solution)/shard_map/project/pallas_call | solution.py:372
  68.6 0.2 collective-permute-start.1
  68.9 2.5 %collective-permute-done.1.got = f32[8,64,512]{2,1,0:T(8,128)S(1)} collective-permute-done((f32[8,64,512]{2,1,0:T(8,128)S(1)}, f32[8,64,512]{2,1,0:T(8,128)S(1)}, u32[]{:S(2)}, u32[]{:S(2)}) %collective-permute-start.1) | collective-permute-done | bytes 1048608 | tf_op jit(solution)/shard_map/ppermute | solution.py:444
  71.4 0.7 pieces_first.1
  72.1 0.1 collective-permute-start.2
  72.2 0.8 collective-permute-start.3
  72.9 2.7 %collective-permute-start.4 = (f32[2,64,256]{2,1,0:T(8,128)S(1)}, f32[2,64,256]{2,1,0:T(8,128)S(1)}, u32[]{:S(2)}, u32[]{:S(2)}) collective-permute-start(f32[2,64,256]{2,1,0:T(8,128)S(1)} %get-tuple-element.25), channel_id=1, source_target_pairs={{0,64},{32,96},{64,0},{96,32},{1,65},{33,97},{65,1},{97,33},{2,66}... | collective-permute-start | bytes 393224 | tf_op jit(solution)/shard_map/ppermute | solution.py:440
  75.6 0.5 collective-permute-start.5
  76.1 2.5 %collective-permute-done.3.x1 = f32[2,64,256]{2,1,0:T(8,128)S(1)} collective-permute-done((f32[2,64,256]{2,1,0:T(8,128)S(1)}, f32[2,64,256]{2,1,0:T(8,128)S(1)}, u32[]{:S(2)}, u32[]{:S(2)}) %collective-permute-start.3) | collective-permute-done | bytes 131104 | tf_op jit(solution)/shard_map/ppermute | solution.py:440
  78.6 2.2 %collective-permute-done.4.x2 = f32[2,64,256]{2,1,0:T(8,128)S(1)} collective-permute-done((f32[2,64,256]{2,1,0:T(8,128)S(1)}, f32[2,64,256]{2,1,0:T(8,128)S(1)}, u32[]{:S(2)}, u32[]{:S(2)}) %collective-permute-start.4) | collective-permute-done | bytes 131104 | tf_op jit(solution)/shard_map/ppermute | solution.py:440
  80.8 1.4 %collective-permute-done.5.x3 = f32[2,64,256]{2,1,0:T(8,128)S(1)} collective-permute-done((f32[2,64,256]{2,1,0:T(8,128)S(1)}, f32[2,64,256]{2,1,0:T(8,128)S(1)}, u32[]{:S(2)}, u32[]{:S(2)}) %collective-permute-start.5) | collective-permute-done | bytes 131104 | tf_op jit(solution)/shard_map/ppermute | solution.py:440
  82.2 0.0 collective-permute-done.2.z_got
  82.2 0.6 pieces_second.1
  82.8 0.6 collective-permute-start.6
  83.5 3.0 %collective-permute-start.7 = (f32[64,256]{1,0:T(8,128)S(1)}, f32[64,256]{1,0:T(8,128)S(1)}, u32[]{:S(2)}, u32[]{:S(2)}) collective-permute-start(f32[64,256]{1,0:T(8,128)S(1)} %get-tuple-element.29), channel_id=1, source_target_pairs={{0,64},{32,96},{64,0},{96,32},{1,65},{33,97},{65,1},{97,33},{2,66}... | collective-permute-start | bytes 196616 | tf_op jit(solution)/shard_map/ppermute | solution.py:440
  86.5 2.0 %collective-permute-start.8 = (f32[64,256]{1,0:T(8,128)S(1)}, f32[64,256]{1,0:T(8,128)S(1)}, u32[]{:S(2)}, u32[]{:S(2)}) collective-permute-start(f32[64,256]{1,0:T(8,128)S(1)} %get-tuple-element.30), channel_id=1, source_target_pairs={{0,96},{32,0},{64,32},{96,64},{1,97},{33,1},{65,33},{97,65},{2,98}... | collective-permute-start | bytes 196616 | tf_op jit(solution)/shard_map/ppermute | solution.py:440
  88.5 1.5 %collective-permute-start.9 = (f32[64,256]{1,0:T(8,128)S(1)}, f32[64,256]{1,0:T(8,128)S(1)}, u32[]{:S(2)}, u32[]{:S(2)}) collective-permute-start(f32[64,256]{1,0:T(8,128)S(1)} %get-tuple-element.32), channel_id=1, source_target_pairs={{0,16},{16,0},{1,17},{17,1},{2,18},{18,2},{3,19},{19,3},{4,20},{20... | collective-permute-start | bytes 196616 | tf_op jit(solution)/shard_map/ppermute | solution.py:463
  90.0 0.0 collective-permute-done.6.y1
  90.0 0.0 collective-permute-done.7.y2
  90.0 0.7 collective-permute-done.8.y3
  90.8 2.0 %collective-permute-done.9.v_got = f32[64,256]{1,0:T(8,128)S(1)} collective-permute-done((f32[64,256]{1,0:T(8,128)S(1)}, f32[64,256]{1,0:T(8,128)S(1)}, u32[]{:S(2)}, u32[]{:S(2)}) %collective-permute-start.9) | collective-permute-done | bytes 65568 | tf_op jit(solution)/shard_map/ppermute | solution.py:463
  92.7 0.7 pieces_third.1
Async XLA Ops:
  1.6 32.1 %copy-start.2 = (s32[136,32]{0,1:T(8,128)S(1)}, s32[136,32]{0,1:T(8,128)}, u32[]{:S(2)}) copy-start(s32[136,32]{0,1:T(8,128)} %param.11) | copy-start | bytes 52228
  1.6 35.1 %copy-start = (f32[64,512]{1,0:T(8,128)S(1)}, f32[64,512]{1,0:T(8,128)}, u32[]{:S(2)}) copy-start(f32[64,512]{1,0:T(8,128)} %tail_hbm.1) | copy-start | bytes 393220
  1.6 35.1 %copy-start.1 = (s32[8,136]{1,0:T(8,128)S(1)}, s32[8,136]{1,0:T(8,128)}, u32[]{:S(2)}) copy-start(s32[8,136]{1,0:T(8,128)} %inv_mask.1) | copy-start | bytes 13060
  33.7 3.0 %collective-permute-start = (f32[8,64,640]{2,1,0:T(8,128)S(1)}, f32[8,64,640]{2,1,0:T(8,128)S(1)}, u32[]{:S(2)}, u32[]{:S(2)}) collective-permute-start(f32[8,64,640]{2,1,0:T(8,128)S(1)} %bitcast.6), channel_id=1, source_target_pairs={{0,8},{8,0},{1,9},{9,1},{2,10},{10,2},{3,11},{11,3},{4,12},{12,4},... | collective-permute-start | bytes 3932168 | tf_op jit(solution)/shard_map/ppermute | solution.py:487
  68.6 2.7 %collective-permute-start.1 = (f32[8,64,512]{2,1,0:T(8,128)S(1)}, f32[8,64,512]{2,1,0:T(8,128)S(1)}, u32[]{:S(2)}, u32[]{:S(2)}) collective-permute-start(f32[8,64,512]{2,1,0:T(8,128)S(1)} %get-tuple-element.20), channel_id=1, source_target_pairs={{0,8},{8,0},{1,9},{9,1},{2,10},{10,2},{3,11},{11,3},{4,12},{12,4},... | collective-permute-start | bytes 3145736 | tf_op jit(solution)/shard_map/ppermute | solution.py:444
  72.1 10.1 %collective-permute-start.2 = (f32[4,64,256]{2,1,0:T(8,128)S(1)}, f32[4,64,256]{2,1,0:T(8,128)S(1)}, u32[]{:S(2)}, u32[]{:S(2)}) collective-permute-start(f32[4,64,256]{2,1,0:T(8,128)S(1)} %get-tuple-element.22), channel_id=1, source_target_pairs={{0,16},{16,0},{1,17},{17,1},{2,18},{18,2},{3,19},{19,3},{4,20},{20... | collective-permute-start | bytes 786440 | tf_op jit(solution)/shard_map/ppermute | solution.py:453
  72.2 6.4 %collective-permute-start.3 = (f32[2,64,256]{2,1,0:T(8,128)S(1)}, f32[2,64,256]{2,1,0:T(8,128)S(1)}, u32[]{:S(2)}, u32[]{:S(2)}) collective-permute-start(f32[2,64,256]{2,1,0:T(8,128)S(1)} %get-tuple-element.24), channel_id=1, source_target_pairs={{0,32},{32,64},{64,96},{96,0},{1,33},{33,65},{65,97},{97,1},{2,34}... | collective-permute-start | bytes 393224 | tf_op jit(solution)/shard_map/ppermute | solution.py:440
  72.9 7.9 %collective-permute-start.4 = (f32[2,64,256]{2,1,0:T(8,128)S(1)}, f32[2,64,256]{2,1,0:T(8,128)S(1)}, u32[]{:S(2)}, u32[]{:S(2)}) collective-permute-start(f32[2,64,256]{2,1,0:T(8,128)S(1)} %get-tuple-element.25), channel_id=1, source_target_pairs={{0,64},{32,96},{64,0},{96,32},{1,65},{33,97},{65,1},{97,33},{2,66}... | collective-permute-start | bytes 393224 | tf_op jit(solution)/shard_map/ppermute | solution.py:440
  75.6 6.6 %collective-permute-start.5 = (f32[2,64,256]{2,1,0:T(8,128)S(1)}, f32[2,64,256]{2,1,0:T(8,128)S(1)}, u32[]{:S(2)}, u32[]{:S(2)}) collective-permute-start(f32[2,64,256]{2,1,0:T(8,128)S(1)} %get-tuple-element.26), channel_id=1, source_target_pairs={{0,96},{32,0},{64,32},{96,64},{1,97},{33,1},{65,33},{97,65},{2,98}... | collective-permute-start | bytes 393224 | tf_op jit(solution)/shard_map/ppermute | solution.py:440
  82.8 7.2 %collective-permute-start.6 = (f32[64,256]{1,0:T(8,128)S(1)}, f32[64,256]{1,0:T(8,128)S(1)}, u32[]{:S(2)}, u32[]{:S(2)}) collective-permute-start(f32[64,256]{1,0:T(8,128)S(1)} %get-tuple-element.28), channel_id=1, source_target_pairs={{0,32},{32,64},{64,96},{96,0},{1,33},{33,65},{65,97},{97,1},{2,34}... | collective-permute-start | bytes 196616 | tf_op jit(solution)/shard_map/ppermute | solution.py:440
  83.5 6.6 %collective-permute-start.7 = (f32[64,256]{1,0:T(8,128)S(1)}, f32[64,256]{1,0:T(8,128)S(1)}, u32[]{:S(2)}, u32[]{:S(2)}) collective-permute-start(f32[64,256]{1,0:T(8,128)S(1)} %get-tuple-element.29), channel_id=1, source_target_pairs={{0,64},{32,96},{64,0},{96,32},{1,65},{33,97},{65,1},{97,33},{2,66}... | collective-permute-start | bytes 196616 | tf_op jit(solution)/shard_map/ppermute | solution.py:440
  86.5 4.3 %collective-permute-start.8 = (f32[64,256]{1,0:T(8,128)S(1)}, f32[64,256]{1,0:T(8,128)S(1)}, u32[]{:S(2)}, u32[]{:S(2)}) collective-permute-start(f32[64,256]{1,0:T(8,128)S(1)} %get-tuple-element.30), channel_id=1, source_target_pairs={{0,96},{32,0},{64,32},{96,64},{1,97},{33,1},{65,33},{97,65},{2,98}... | collective-permute-start | bytes 196616 | tf_op jit(solution)/shard_map/ppermute | solution.py:440
  88.5 4.3 %collective-permute-start.9 = (f32[64,256]{1,0:T(8,128)S(1)}, f32[64,256]{1,0:T(8,128)S(1)}, u32[]{:S(2)}, u32[]{:S(2)}) collective-permute-start(f32[64,256]{1,0:T(8,128)S(1)} %get-tuple-element.32), channel_id=1, source_target_pairs={{0,16},{16,0},{1,17},{17,1},{2,18},{18,2},{3,19},{19,3},{4,20},{20... | collective-permute-start | bytes 196616 | tf_op jit(solution)/shard_map/ppermute | solution.py:463

commit v3 on v2

--- a/solution.py
+++ b/solution.py
@@ -131,7 +131,7 @@
     where_ref, inv_mask, ks_mask, mine_ref, other_ref, coupling_hbm, lead_hbm, tail_hbm,
     kept_ref, sent_ref,
     m_ref, coupling_ref, lead_ref, tail_ref, c_ref, k_ref, t_ref, x_ref, lead_stack,
-    before_ref, right_even, right_odd, left_ref, lines_ref, last_ref, sem, strip_sem,
+    before_ref, right_even, right_odd, left_ref, lines_ref, last_ref, sem,
 ):
     right_refs = (right_even, right_odd)
     size = m_ref.shape[0]
@@ -154,46 +154,29 @@
     def at(i):
         return slice(i * BLK, (i + 1) * BLK)
 
-    strips = {b: [] for b in range(count)}
-    folds = {b: [] for b in range(count)}
-    sems = iter(range(strip_sem.shape[0]))
-    for b in range(count):
+    def place(b):
         for ref, part in ((mine_ref, core), (other_ref, 1 - core)):
             held = pl.ds(pl.multiple_of(b * BLK + part * 64, 64), 64)
             direct = min(SENT, count - b) * BLK
-            strips[b].append(
-                pltpu.make_async_copy(
-                    ref.at[b, :, pl.ds(0, direct)],
-                    m_ref.at[held, pl.ds(b * BLK, direct)],
-                    strip_sem.at[next(sems)],
-                )
-            )
+            m_ref[held, b * BLK : b * BLK + direct] = ref[b, :, :direct]
             for o in range(count - b, SENT - 1):
-                c = b + o - count
-                strips[b].append(
-                    pltpu.make_async_copy(
-                        ref.at[b, :, pl.ds(o * BLK, BLK)],
-                        m_ref.at[held, pl.ds(c * BLK, BLK)],
-                        strip_sem.at[next(sems)],
-                    )
-                )
-    for b in range(count):
-        for copy in strips[b]:
-            copy.start()
+                m_ref[held, at(b + o - count)] = ref[b, :, at(o)]
+
     tail_copy.start()
     for k in range(count):
         lead_copies[k].start()
     for k in range(count):
         coupling_copies[k].start()
     lines_ref[...] = jnp.zeros(lines_ref.shape, BF16)
-    for copy in strips[0]:
-        copy.wait()
+    place(0)
 
     def arrive():
-        for b in range(1, count):
-            for copy in strips[b]:
-                copy.wait()
-        yield
+        for b in range(SENT, count):
+            place(b)
+            yield
+        for b in range(1, SENT):
+            place(b)
+            yield
         for b in range(SENT, count):
             for c in range(b - SENT + 1):
                 m_ref[at(c), at(b)] = m_ref[at(b), at(c)].T
@@ -318,7 +301,7 @@
             sent_ref[i, :, wide] = jnp.where(core == 0, total[half:], total[:half])
             yield
 
-    fillers = [arrive(), prepare_row(0), pause(6), prepare(), split_coupling(0)]
+    fillers = [arrive(), prepare_row(0), pause(2), prepare(), split_coupling(0)]
     for j in range(count):
         rows = [m_ref[j * BLK + 8 * g : j * BLK + 8 * g + 8, at(j)] for g in range(16)]
         for step in factor_panels(rows, sub, lane, lines_ref):
@@ -372,7 +355,7 @@
     return pl.pallas_call(
         kernel,
         out_shape=[jax.ShapeDtypeStruct((size // BLK, BLK // 2, width), F32)] * 2,
-        in_specs=[smem, smem, smem, hbm, hbm, hbm, hbm, hbm],
+        in_specs=[smem, smem, smem, vmem, vmem, hbm, hbm, hbm],
         out_specs=[vmem, vmem],
         scratch_shapes=[
             pltpu.VMEM((size, size), F32),
@@ -391,7 +374,6 @@
             pltpu.VMEM((5, 3 * BLK, BLK), BF16),
             pltpu.VMEM((3 * BLK, size), BF16),
             pltpu.SemaphoreType.DMA((17,)),
-            pltpu.SemaphoreType.DMA((28,)),
         ],
         compiler_params=pltpu.CompilerParams(vmem_limit_bytes=48 * 1024 * 1024),
         name="project",

time: 93.7 us -> 93 us (level)
  no operation moved by 1% of the time
where the time goes in v3:
time: 93 us; the launch traced here: 92.7 us
  Pallas kernels  33.1 us (36%)
  blocking collectives  32.1 us (35%)
  waiting for transfers between devices  14.2 us (15%)
  starting transfers between devices  11.4 us (12%)
  local copies, waits for them, and re-layouts  1.01 us (1%)
    all_to_all x1, blocking collectives, per_device(): lax.all_to_all(copies, CHIPS, split_axis=0, concat_axis=0, tiled=True)  32.1 us
    pallas_call x1, Pallas kernels, projected_part(): pl.pallas_call(kernel, out_shape=[jax.ShapeDtypeStruct((size // BLK, BLK...  31.2 us
    ppermute x6, starting transfers between devices, turned(): lax.ppermute(part, 'row_0', [(s, (s + k) % 4) for s in range(4)])  9.6 us
    ppermute x6, waiting for transfers between devices, turned(): lax.ppermute(part, 'row_0', [(s, (s + k) % 4) for s in range(4)])  6.83 us
    ppermute x1, waiting for transfers between devices, per_device(): other = lax.ppermute(mine, 'row_2', [(0, 1), (1, 0)])  2.84 us
    ppermute x1, waiting for transfers between devices, summed(): got = lax.ppermute(sent, 'row_2', swap)  2.53 us
    ppermute x1, waiting for transfers between devices, summed(): v_got = lax.ppermute(v_sent, 'row_1', swap)  1.99 us
  transfers between devices with their start and end apart: 10, of which 7 were waited for; matrix products, arithmetic and copies ran while one was open for 0% of the time, Pallas kernels for 0%

profile of v3, /device:TPU:2, one launch (start us, length us, event | category | flops | bytes accessed | tf_op | source)
XLA Modules:
  0.0 92.7 jit_solution(167503604238418252)
XLA Ops:
  0.0 0.7 slice.3
  0.7 0.7 fusion
  1.5 0.1 broadcast_in_dim.2
  1.6 0.0 copy-start.2
  1.6 0.0 copy-start
  1.6 0.0 copy-start.1
  1.6 32.1 %all_to_all.5 = f32[64,8,640]{2,1,0:T(8,128)S(1)} all-to-all(f32[64,8,640]{2,1,0:T(8,128)S(1)} %broadcast_in_dim.2), channel_id=1, replica_groups=mesh['row_0'=4,'row_1'=2,'row_2'=2,'col_0'=4,'col_1'=2] {'row_0','row_1'..., dimensions={0} | all-to-all | bytes 2621440 | tf_op jit(solution)/shard_map/all_to_all | solution.py:467
  33.7 0.0 collective-permute-start
  33.7 0.0 copy-done.2
  33.7 0.1 copy.7.ks_mask
  33.8 0.1 stack.23.where_ref
  33.9 2.8 %collective-permute-done.other_ref = f32[8,64,640]{2,1,0:T(8,128)S(1)} collective-permute-done((f32[8,64,640]{2,1,0:T(8,128)S(1)}, f32[8,64,640]{2,1,0:T(8,128)S(1)}, u32[]{:S(2)}, u32[]{:S(2)}) %collective-permute-start) | collective-permute-done | bytes 1310752 | tf_op jit(solution)/shard_map/ppermute | solution.py:469
  36.7 0.0 copy-done
  36.7 0.0 copy-done.1
  36.7 31.2 %project.1 = (f32[8,64,512]{2,1,0:T(8,128)S(1)}, f32[8,64,512]{2,1,0:T(8,128)S(1)}) custom-call(s32[5]{0:T(128)S(1)} %stack.23.where_ref, s32[8,136]{1,0:T(8,128)S(1)} %copy-done.1, s32[136,32]{1,0:T(8,128)S(1)} %copy.7.ks_mask, f32[8,64,640]{2,1,0:T(8,128)S(1)} %bitcast.7, f32[8,64,640]{2,1,0:T(8,128)S(1)} %collective-permute-done.other_ref, ...), custom_call_target="tpu_custom_call" | custom-call | tf_op jit(solution)/shard_map/project/pallas_call | solution.py:355
  67.9 0.2 collective-permute-start.1
  68.1 2.5 %collective-permute-done.1.got = f32[8,64,512]{2,1,0:T(8,128)S(1)} collective-permute-done((f32[8,64,512]{2,1,0:T(8,128)S(1)}, f32[8,64,512]{2,1,0:T(8,128)S(1)}, u32[]{:S(2)}, u32[]{:S(2)}) %collective-permute-start.1) | collective-permute-done | bytes 1048608 | tf_op jit(solution)/shard_map/ppermute | solution.py:426
  70.6 0.7 pieces_first.1
  71.3 0.1 collective-permute-start.2
  71.4 0.7 collective-permute-start.3
  72.2 2.7 %collective-permute-start.4 = (f32[2,64,256]{2,1,0:T(8,128)S(1)}, f32[2,64,256]{2,1,0:T(8,128)S(1)}, u32[]{:S(2)}, u32[]{:S(2)}) collective-permute-start(f32[2,64,256]{2,1,0:T(8,128)S(1)} %get-tuple-element.25), channel_id=1, source_target_pairs={{0,64},{32,96},{64,0},{96,32},{1,65},{33,97},{65,1},{97,33},{2,66}... | collective-permute-start | bytes 393224 | tf_op jit(solution)/shard_map/ppermute | solution.py:422
  74.9 0.5 collective-permute-start.5
  75.4 2.5 %collective-permute-done.3.x1 = f32[2,64,256]{2,1,0:T(8,128)S(1)} collective-permute-done((f32[2,64,256]{2,1,0:T(8,128)S(1)}, f32[2,64,256]{2,1,0:T(8,128)S(1)}, u32[]{:S(2)}, u32[]{:S(2)}) %collective-permute-start.3) | collective-permute-done | bytes 131104 | tf_op jit(solution)/shard_map/ppermute | solution.py:422
  77.9 2.2 %collective-permute-done.4.x2 = f32[2,64,256]{2,1,0:T(8,128)S(1)} collective-permute-done((f32[2,64,256]{2,1,0:T(8,128)S(1)}, f32[2,64,256]{2,1,0:T(8,128)S(1)}, u32[]{:S(2)}, u32[]{:S(2)}) %collective-permute-start.4) | collective-permute-done | bytes 131104 | tf_op jit(solution)/shard_map/ppermute | solution.py:422
  80.0 1.4 %collective-permute-done.5.x3 = f32[2,64,256]{2,1,0:T(8,128)S(1)} collective-permute-done((f32[2,64,256]{2,1,0:T(8,128)S(1)}, f32[2,64,256]{2,1,0:T(8,128)S(1)}, u32[]{:S(2)}, u32[]{:S(2)}) %collective-permute-start.5) | collective-permute-done | bytes 131104 | tf_op jit(solution)/shard_map/ppermute | solution.py:422
  81.5 0.0 collective-permute-done.2.z_got
  81.5 0.6 pieces_second.1
  82.1 0.6 collective-permute-start.6
  82.7 3.0 %collective-permute-start.7 = (f32[64,256]{1,0:T(8,128)S(1)}, f32[64,256]{1,0:T(8,128)S(1)}, u32[]{:S(2)}, u32[]{:S(2)}) collective-permute-start(f32[64,256]{1,0:T(8,128)S(1)} %get-tuple-element.29), channel_id=1, source_target_pairs={{0,64},{32,96},{64,0},{96,32},{1,65},{33,97},{65,1},{97,33},{2,66}... | collective-permute-start | bytes 196616 | tf_op jit(solution)/shard_map/ppermute | solution.py:422
  85.8 2.0 %collective-permute-start.8 = (f32[64,256]{1,0:T(8,128)S(1)}, f32[64,256]{1,0:T(8,128)S(1)}, u32[]{:S(2)}, u32[]{:S(2)}) collective-permute-start(f32[64,256]{1,0:T(8,128)S(1)} %get-tuple-element.30), channel_id=1, source_target_pairs={{0,96},{32,0},{64,32},{96,64},{1,97},{33,1},{65,33},{97,65},{2,98}... | collective-permute-start | bytes 196616 | tf_op jit(solution)/shard_map/ppermute | solution.py:422
  87.7 1.5 %collective-permute-start.9 = (f32[64,256]{1,0:T(8,128)S(1)}, f32[64,256]{1,0:T(8,128)S(1)}, u32[]{:S(2)}, u32[]{:S(2)}) collective-permute-start(f32[64,256]{1,0:T(8,128)S(1)} %get-tuple-element.32), channel_id=1, source_target_pairs={{0,16},{16,0},{1,17},{17,1},{2,18},{18,2},{3,19},{19,3},{4,20},{20... | collective-permute-start | bytes 196616 | tf_op jit(solution)/shard_map/ppermute | solution.py:445
  89.3 0.0 collective-permute-done.6.y1
  89.3 0.0 collective-permute-done.7.y2
  89.3 0.7 collective-permute-done.8.y3
  90.0 2.0 %collective-permute-done.9.v_got = f32[64,256]{1,0:T(8,128)S(1)} collective-permute-done((f32[64,256]{1,0:T(8,128)S(1)}, f32[64,256]{1,0:T(8,128)S(1)}, u32[]{:S(2)}, u32[]{:S(2)}) %collective-permute-start.9) | collective-permute-done | bytes 65568 | tf_op jit(solution)/shard_map/ppermute | solution.py:445
  92.0 0.7 pieces_third.1
Async XLA Ops:
  1.6 32.1 %copy-start.2 = (s32[136,32]{0,1:T(8,128)S(1)}, s32[136,32]{0,1:T(8,128)}, u32[]{:S(2)}) copy-start(s32[136,32]{0,1:T(8,128)} %param.11) | copy-start | bytes 52228
  1.6 35.1 %copy-start = (f32[64,512]{1,0:T(8,128)S(1)}, f32[64,512]{1,0:T(8,128)}, u32[]{:S(2)}) copy-start(f32[64,512]{1,0:T(8,128)} %tail_hbm.1) | copy-start | bytes 393220
  1.6 35.1 %copy-start.1 = (s32[8,136]{1,0:T(8,128)S(1)}, s32[8,136]{1,0:T(8,128)}, u32[]{:S(2)}) copy-start(s32[8,136]{1,0:T(8,128)} %inv_mask.1) | copy-start | bytes 13060
  33.7 3.0 %collective-permute-start = (f32[8,64,640]{2,1,0:T(8,128)S(1)}, f32[8,64,640]{2,1,0:T(8,128)S(1)}, u32[]{:S(2)}, u32[]{:S(2)}) collective-permute-start(f32[8,64,640]{2,1,0:T(8,128)S(1)} %bitcast.6), channel_id=1, source_target_pairs={{0,8},{8,0},{1,9},{9,1},{2,10},{10,2},{3,11},{11,3},{4,12},{12,4},... | collective-permute-start | bytes 3932168 | tf_op jit(solution)/shard_map/ppermute | solution.py:469
  67.9 2.7 %collective-permute-start.1 = (f32[8,64,512]{2,1,0:T(8,128)S(1)}, f32[8,64,512]{2,1,0:T(8,128)S(1)}, u32[]{:S(2)}, u32[]{:S(2)}) collective-permute-start(f32[8,64,512]{2,1,0:T(8,128)S(1)} %get-tuple-element.20), channel_id=1, source_target_pairs={{0,8},{8,0},{1,9},{9,1},{2,10},{10,2},{3,11},{11,3},{4,12},{12,4},... | collective-permute-start | bytes 3145736 | tf_op jit(solution)/shard_map/ppermute | solution.py:426
  71.3 10.1 %collective-permute-start.2 = (f32[4,64,256]{2,1,0:T(8,128)S(1)}, f32[4,64,256]{2,1,0:T(8,128)S(1)}, u32[]{:S(2)}, u32[]{:S(2)}) collective-permute-start(f32[4,64,256]{2,1,0:T(8,128)S(1)} %get-tuple-element.22), channel_id=1, source_target_pairs={{0,16},{16,0},{1,17},{17,1},{2,18},{18,2},{3,19},{19,3},{4,20},{20... | collective-permute-start | bytes 786440 | tf_op jit(solution)/shard_map/ppermute | solution.py:435
  71.4 6.4 %collective-permute-start.3 = (f32[2,64,256]{2,1,0:T(8,128)S(1)}, f32[2,64,256]{2,1,0:T(8,128)S(1)}, u32[]{:S(2)}, u32[]{:S(2)}) collective-permute-start(f32[2,64,256]{2,1,0:T(8,128)S(1)} %get-tuple-element.24), channel_id=1, source_target_pairs={{0,32},{32,64},{64,96},{96,0},{1,33},{33,65},{65,97},{97,1},{2,34}... | collective-permute-start | bytes 393224 | tf_op jit(solution)/shard_map/ppermute | solution.py:422
  72.2 7.9 %collective-permute-start.4 = (f32[2,64,256]{2,1,0:T(8,128)S(1)}, f32[2,64,256]{2,1,0:T(8,128)S(1)}, u32[]{:S(2)}, u32[]{:S(2)}) collective-permute-start(f32[2,64,256]{2,1,0:T(8,128)S(1)} %get-tuple-element.25), channel_id=1, source_target_pairs={{0,64},{32,96},{64,0},{96,32},{1,65},{33,97},{65,1},{97,33},{2,66}... | collective-permute-start | bytes 393224 | tf_op jit(solution)/shard_map/ppermute | solution.py:422
  74.9 6.6 %collective-permute-start.5 = (f32[2,64,256]{2,1,0:T(8,128)S(1)}, f32[2,64,256]{2,1,0:T(8,128)S(1)}, u32[]{:S(2)}, u32[]{:S(2)}) collective-permute-start(f32[2,64,256]{2,1,0:T(8,128)S(1)} %get-tuple-element.26), channel_id=1, source_target_pairs={{0,96},{32,0},{64,32},{96,64},{1,97},{33,1},{65,33},{97,65},{2,98}... | collective-permute-start | bytes 393224 | tf_op jit(solution)/shard_map/ppermute | solution.py:422
  82.1 7.2 %collective-permute-start.6 = (f32[64,256]{1,0:T(8,128)S(1)}, f32[64,256]{1,0:T(8,128)S(1)}, u32[]{:S(2)}, u32[]{:S(2)}) collective-permute-start(f32[64,256]{1,0:T(8,128)S(1)} %get-tuple-element.28), channel_id=1, source_target_pairs={{0,32},{32,64},{64,96},{96,0},{1,33},{33,65},{65,97},{97,1},{2,34}... | collective-permute-start | bytes 196616 | tf_op jit(solution)/shard_map/ppermute | solution.py:422
  82.7 6.6 %collective-permute-start.7 = (f32[64,256]{1,0:T(8,128)S(1)}, f32[64,256]{1,0:T(8,128)S(1)}, u32[]{:S(2)}, u32[]{:S(2)}) collective-permute-start(f32[64,256]{1,0:T(8,128)S(1)} %get-tuple-element.29), channel_id=1, source_target_pairs={{0,64},{32,96},{64,0},{96,32},{1,65},{33,97},{65,1},{97,33},{2,66}... | collective-permute-start | bytes 196616 | tf_op jit(solution)/shard_map/ppermute | solution.py:422
  85.8 4.3 %collective-permute-start.8 = (f32[64,256]{1,0:T(8,128)S(1)}, f32[64,256]{1,0:T(8,128)S(1)}, u32[]{:S(2)}, u32[]{:S(2)}) collective-permute-start(f32[64,256]{1,0:T(8,128)S(1)} %get-tuple-element.30), channel_id=1, source_target_pairs={{0,96},{32,0},{64,32},{96,64},{1,97},{33,1},{65,33},{97,65},{2,98}... | collective-permute-start | bytes 196616 | tf_op jit(solution)/shard_map/ppermute | solution.py:422
  87.7 4.3 %collective-permute-start.9 = (f32[64,256]{1,0:T(8,128)S(1)}, f32[64,256]{1,0:T(8,128)S(1)}, u32[]{:S(2)}, u32[]{:S(2)}) collective-permute-start(f32[64,256]{1,0:T(8,128)S(1)} %get-tuple-element.32), channel_id=1, source_target_pairs={{0,16},{16,0},{1,17},{17,1},{2,18},{18,2},{3,19},{19,3},{4,20},{20... | collective-permute-start | bytes 196616 | tf_op jit(solution)/shard_map/ppermute | solution.py:445
